TPU v7x, 128 devices: a whole 4x4x4 slice. The times are simulated.
128 devices in a mesh: row: 16 (over z, y_hi, core), col: 8 (over y_lo, x).
Axes of the slice: x: 4, y: 4 (y_hi: 2, y_lo: 2; y = y_hi * 2 + y_lo), z: 4, core: 2. Of those that a mesh axis runs over, the one named last changes fastest.
Arguments:
- fine_residual: float32 [16, 3, 6291456], P(None, None, ('row', 'col')), may hold values from -6 to 6
- restriction: float32 [3, 3, 6291456], P(None, None, ('row', 'col')), may hold values from -1.25 to 1.25
- restriction_pattern: int32 [6291456], P(('row', 'col')), may hold values 0 or 1
- cell_aggregate: int32 [768, 1024], P('row', 'col'), may hold values from 0 to 786431, as said below
- block_inverse: float32 [3, 3, 768, 1024], P(None, None, 'row', 'col'), may hold values from -4 to 4, as said below
- off_blocks: float32 [4, 3, 3, 768, 1024], P(None, None, None, 'row', 'col'), may hold values from -0.5 to 0.5
- operator_pattern: int32 [4, 768, 1024], P(None, 'row', 'col'), may hold values 0 or 1
Outputs:
- coarse_solution: float32 [16, 3, 768, 1024], P(None, None, 'row', 'col')
- fine_correction: float32 [16, 3, 6291456], P(None, None, ('row', 'col'))
Inputs may be any that keep to these rules, and one draw needn't show every extreme that they name: `cell_aggregate`: every aggregate number 0 to 786431 stands in exactly one coarse cell. Aggregate g = f * 6144 + a lies in the tile numbered a mod 128, where the tile of rows i * 48 to (i + 1) * 48 - 1 and columns j * 128 to (j + 1) * 128 - 1 is numbered i * 8 + j. `block_inverse`: each 3x3 block is the inverse of a cell's diagonal block.
All inputs are finite; a program needn't handle non-finite values. No bound on the sum of `restriction_pattern` or of `operator_pattern` on one device may be relied on, other than what follows from the above.
Results may differ from a plain program's by a relative error of at most 0.00002.
Values sent between devices are 32-bit elements; how exact they have to be, the bound alone decides.
A program may use at most 128 MiB of HBM per device.

v0:
```python
import functools

import jax
import jax.numpy as jnp
from jax import lax
from jax.experimental import pallas as pl
from jax.experimental.pallas import tpu as pltpu
from jax.sharding import PartitionSpec as P

MESH = pl.DeviceIdType.MESH
ND = 128
NQ = 16
NI = 48
NK = 48
W = 48
AGG = 6144
FPA = 8
CHUNKS = 3
LANES = 128
F32 = jnp.float32


def me_index():
    return lax.axis_index("row") * 8 + lax.axis_index("col")


def coords(p):
    return (p // 8, p % 8)


def lane_ids():
    return lax.broadcasted_iota(jnp.int32, (8, LANES), 1)


def bcast_row(ref, *idx):
    return jnp.broadcast_to(ref[idx], (8, LANES))


def start_barrier():
    bar = pltpu.get_barrier_semaphore()
    me = me_index()

    def sig(o, c):
        p = lax.rem(me + o, ND)
        pl.semaphore_signal(bar, inc=1, device_id=coords(p), device_id_type=MESH)
        return c

    lax.fori_loop(1, ND, sig, 0)


def end_barrier():
    pl.semaphore_wait(pltpu.get_barrier_semaphore(), ND - 1)


def send_chunk(S, R, b, ssem, rsem):
    me = me_index()

    def send(o, c):
        p = lax.rem(me + o, ND)
        pltpu.make_async_remote_copy(
            S.at[b, p, pl.ds(0, 6)],
            R.at[b, me, pl.ds(0, 6)],
            ssem.at[b],
            rsem.at[b],
            device_id=coords(p),
            device_id_type=MESH,
        ).start()
        return c

    lax.fori_loop(1, ND, send, 0)


def wait_chunk(R, b, sem):
    block = R.at[b, pl.ds(0, ND - 1), pl.ds(0, 6)]
    pltpu.make_async_copy(block, block, sem.at[b]).wait()


def keep_own(S, R, b):
    me = me_index()
    R[b, me] = S[b, me]


def restrict_chunk(b, r, w, pat, A):
    def one(kk, c):
        k = b * 16 + kk
        acc = [[None] * 2 for _ in range(3)]
        for p in range(FPA):
            n = pl.multiple_of(p * AGG + k * LANES, LANES)
            there = bcast_row(pat, pl.ds(p * 48 + k, 1), slice(None)).astype(F32)
            here = [
                [r[j, qg * 8 : qg * 8 + 8, pl.ds(n, LANES)] * there for qg in range(2)]
                for j in range(3)
            ]
            for i in range(3):
                for j in range(3):
                    wij = jnp.broadcast_to(w[i, j : j + 1, pl.ds(n, LANES)], (8, LANES))
                    for qg in range(2):
                        term = wij * here[j][qg]
                        acc[i][qg] = term if acc[i][qg] is None else acc[i][qg] + term
        for i in range(3):
            for qg in range(2):
                at = pl.multiple_of(k * W + i * 16 + qg * 8, 8)
                A[pl.ds(at, 8), :] = acc[i][qg]
        return c

    lax.fori_loop(0, 16, one, 0)


def pack_chunk(b, A, S2d):
    for h in range(2):
        k8 = b * 16 + 8 * h
        six, seven = (k8 + 6) * W, (k8 + 7) * W
        for m in range(3):
            at = (k8 + 2 * m) * W
            head = A[at : at + 96, :]
            if m == 0:
                tail = [A[six : six + 32, :]]
            elif m == 1:
                tail = [A[seven : seven + 32, :]]
            else:
                tail = [A[six + 32 : six + 48, :], A[seven + 32 : seven + 48, :]]
            turned = jnp.concatenate([head] + tail, axis=0).T
            for t0 in range(16):
                rows = pl.ds(b * 1024 + t0 * 64 + 2 * m + h, 8, stride=8)
                S2d[rows, :] = turned[t0 * 8 : t0 * 8 + 8, :]


def unfold_chunk(b, R2d):
    lane = lane_ids()

    def one(fb, c):
        base = b * 1024 + fb * 64
        for h in range(2):
            x0 = R2d[pl.ds(base + h, 8, stride=8), :]
            x1 = R2d[pl.ds(base + 2 + h, 8, stride=8), :]
            x2 = R2d[pl.ds(base + 4 + h, 8, stride=8), :]
            six = jnp.where(lane < 32, pltpu.roll(x0, 32, 1), pltpu.roll(x2, 64, 1))
            seven = jnp.where(lane < 80, pltpu.roll(x1, 80, 1), pltpu.roll(x2, 96, 1))
            R2d[pl.ds(base + 6 + h, 8, stride=8), :] = jnp.where(lane < 48, six, seven)
        return c

    lax.fori_loop(0, 16, one, 0)


def fold_chunk(b, S2d):
    lane = lane_ids()

    def one(fb, c):
        base = b * 1024 + fb * 64
        for h in range(2):
            d = S2d[pl.ds(base + 6 + h, 8, stride=8), :]
            late = lane >= 96
            for m, moved in enumerate(
                (
                    pltpu.roll(d, 96, 1),
                    pltpu.roll(d, 48, 1),
                    jnp.where(lane < 112, pltpu.roll(d, 64, 1), pltpu.roll(d, 32, 1)),
                )
            ):
                rows = pl.ds(base + 2 * m + h, 8, stride=8)
                S2d[rows, :] = jnp.where(late, moved, S2d[rows, :])
        return c

    lax.fori_loop(0, 16, one, 0)


def gather_rows(slot, R2d, G):
    def some(blk, c):
        for u in range(64):
            c0 = blk * 64 + u
            G[pl.ds(c0, 1), :] = R2d[pl.ds(slot[c0], 1), :]
        return c

    lax.fori_loop(0, AGG // 64, some, 0)


def cells_to_planes(G, odd, rhs):
    def one(two, c):
        for u in range(4):
            row = two * 4 + u
            at = pl.multiple_of(row * LANES, LANES)
            turned = G[pl.ds(at, LANES), :].T
            is_odd = bcast_row(odd, pl.ds(row, 1), slice(None)) == 1
            for v in range(6):
                here = jnp.where(
                    is_odd, turned[W + v * 8 : W + v * 8 + 8, :], turned[v * 8 : v * 8 + 8, :]
                )
                rhs[pl.ds(pl.multiple_of(row * W + v * 8, 8), 8), :] = here
        return c

    lax.fori_loop(0, NI // 4, one, 0)


def solve_block(binv, row, total):
    out = []
    for i in range(3):
        acc = None
        for j in range(3):
            coef = bcast_row(binv, i * 3 + j, pl.ds(row, 1), slice(None))
            terms = [coef * total[j][qg] for qg in range(2)]
            acc = terms if acc is None else [x + y for x, y in zip(acc, terms)]
        out.append(acc)
    return out


def first_sweep(rhs, binv, X):
    def one(row, c):
        base = pl.multiple_of(row * W, 8)
        total = [
            [rhs[pl.ds(base + j * 16 + qg * 8, 8), :] for qg in range(2)] for j in range(3)
        ]
        new = solve_block(binv, row, total)
        for i in range(3):
            for qg in range(2):
                X[0, pl.ds(base + W + i * 16 + qg * 8, 8), :] = new[i][qg]
        return c

    lax.fori_loop(0, NI, one, 0)


def shift_columns(s, X, XL, XR, PL, PR):
    lane = lane_ids()

    def one(blk, carry):
        left, right = carry
        left, right = list(left), list(right)
        for u in range(4):
            row = blk * 4 + u
            base = pl.multiple_of(row * W, 8)
            for v in range(6):
                x = X[s, pl.ds(base + W + v * 8, 8), :]
                XL[pl.ds(base + v * 8, 8), :] = pltpu.roll(x, 1, 1)
                XR[pl.ds(base + v * 8, 8), :] = pltpu.roll(x, LANES - 1, 1)
                first = jnp.broadcast_to(x[:, 0:1], (8, LANES))
                last = jnp.broadcast_to(x[:, LANES - 1 : LANES], (8, LANES))
                left[v] = jnp.where(lane == row, first, left[v])
                right[v] = jnp.where(lane == row, last, right[v])
        return tuple(left), tuple(right)

    zero = tuple(jnp.zeros((8, LANES), F32) for _ in range(6))
    left, right = lax.fori_loop(0, NI // 4, one, (zero, zero))
    for v in range(6):
        PL[s, v * 8 : v * 8 + 8, :] = left[v]
        PR[s, v * 8 : v * 8 + 8, :] = right[v]


def halo_copies(s, X, PL, PR, HL, HR, hs, hr):
    row, col = lax.axis_index("row"), lax.axis_index("col")
    own_first = X.at[s, pl.ds(W, W)]
    own_last = X.at[s, pl.ds(NI * W, W)]
    above = X.at[s, pl.ds(0, W)]
    below = X.at[s, pl.ds((NI + 1) * W, W)]
    table = [
        (row > 0, row < 15, own_first, below, (row - 1, col), 0),
        (row < 15, row > 0, own_last, above, (row + 1, col), 1),
        (col > 0, col < 7, PL.at[s], HR.at[s], (row, col - 1), 2),
        (col < 7, col > 0, PR.at[s], HL.at[s], (row, col + 1), 3),
    ]
    return [
        (
            sends,
            receives,
            pltpu.make_async_remote_copy(
                src, dst, hs.at[s, n], hr.at[s, n], device_id=dev, device_id_type=MESH
            ),
            dst,
        )
        for sends, receives, src, dst, dev, n in table
    ]


def exchange_halo(s, X, PL, PR, HL, HR, hs, hr):
    copies = halo_copies(s, X, PL, PR, HL, HR, hs, hr)
    for sends, _, copy, _ in copies:
        pl.when(sends)(copy.start)
    for _, receives, copy, dst in copies:
        pl.when(receives)(copy.wait_recv)

        def clear(dst=dst):
            dst[...] = jnp.zeros((W, LANES), F32)

        pl.when(jnp.logical_not(receives))(clear)


def fill_columns(s, XL, XR, HL, HR):
    lane = lane_ids()

    def one(blk, c):
        for u in range(4):
            row = blk * 4 + u
            base = pl.multiple_of(row * W, 8)
            for v in range(6):
                at = pl.ds(base + v * 8, 8)
                edge = pltpu.roll(HL[s, v * 8 : v * 8 + 8, :], LANES - row, 1)
                XL[at, :] = jnp.where(lane == 0, edge, XL[at, :])
                edge = pltpu.roll(HR[s, v * 8 : v * 8 + 8, :], LANES - 1 - row, 1)
                XR[at, :] = jnp.where(lane == LANES - 1, edge, XR[at, :])
        return c

    lax.fori_loop(0, NI // 4, one, 0)


def sweep(s, rhs, binv, coup, X, XL, XR, out):
    def one(row, c):
        base = pl.multiple_of(row * W, 8)

        def at(v):
            return pl.ds(base + v * 8, 8)

        total = [[rhs[at(j * 2 + qg), :] for qg in range(2)] for j in range(3)]
        for d in range(4):
            for k in range(3):
                near = []
                for qg in range(2):
                    v = k * 2 + qg
                    if d == 0:
                        near.append(X[s, at(v), :])
                    elif d == 1:
                        near.append(X[s, at(v + 12), :])
                    elif d == 2:
                        near.append(XL[at(v), :])
                    else:
                        near.append(XR[at(v), :])
                for j in range(3):
                    coef = bcast_row(coup, d * 9 + j * 3 + k, pl.ds(row, 1), slice(None))
                    for qg in range(2):
                        total[j][qg] = total[j][qg] - coef * near[qg]
        new = solve_block(binv, row, total)
        for i in range(3):
            for qg in range(2):
                v = i * 2 + qg
                if out is None:
                    X[s + 1, at(v + 6), :] = new[i][qg]
                else:
                    planes, last = out
                    last[at(v), :] = new[i][qg]
                    planes[pl.ds((qg * 8 * 3 + i) * NI + row, 8, stride=3 * NI), :] = new[i][qg]
        return c

    lax.fori_loop(0, NI, one, 0)


def planes_to_cells(last, G):
    def one(blk, c):
        for u in range(4):
            row = blk * 4 + u
            x = last[pl.ds(pl.multiple_of(row * W, 8), W), :]
            turned = jnp.concatenate([x, x, x[0:32]], axis=0).T
            G[pl.ds(pl.multiple_of(row * LANES, LANES), LANES), :] = turned
        return c

    lax.fori_loop(0, NI // 4, one, 0)


def collect_chunk(b, inv, G, S2d):
    lane = lax.broadcasted_iota(jnp.int32, (1, LANES), 1)

    def one(fb, c):
        for u in range(4):
            f = fb * 4 + u
            for rr in range(8):
                even = G[pl.ds(inv[(b * ND + f) * 16 + rr * 2], 1), :]
                odd = G[pl.ds(inv[(b * ND + f) * 16 + rr * 2 + 1], 1), :]
                S2d[pl.ds(b * 1024 + f * 8 + rr, 1), :] = jnp.where(lane < W, even, odd)
        return c

    lax.fori_loop(0, ND // 4, one, 0)


def spread_chunk(b, R2d, Y):
    for h in range(2):
        k8 = b * 16 + 8 * h
        six, seven = (k8 + 6) * W, (k8 + 7) * W
        for m in range(3):
            parts = [
                R2d[pl.ds(b * 1024 + t0 * 64 + 2 * m + h, 8, stride=8), :] for t0 in range(16)
            ]
            turned = jnp.concatenate(parts, axis=0).T
            at = (k8 + 2 * m) * W
            Y[at : at + 96, :] = turned[0:96]
            if m == 0:
                Y[six : six + 32, :] = turned[96:128]
            elif m == 1:
                Y[seven : seven + 32, :] = turned[96:128]
            else:
                Y[six + 32 : six + 48, :] = turned[96:112]
                Y[seven + 32 : seven + 48, :] = turned[112:128]


def coarse_kernel(
    slot,
    inv,
    r_hbm,
    w_hbm,
    pat,
    odd,
    binv,
    off,
    opat,
    planes,
    Y,
    r,
    w,
    A,
    S,
    R,
    S2,
    R2,
    G,
    rhs,
    X,
    XL,
    XR,
    PL,
    PR,
    HL,
    HR,
    coup,
    load_sem,
    s1,
    r1,
    s2,
    r2,
    hs,
    hr,
):
    loads = []
    for b in range(CHUNKS):
        for p in range(FPA):
            n = pl.ds(p * AGG + b * 2048, 2048)
            loads.append((b, r_hbm.at[:, :, n], r.at[:, :, n], load_sem.at[0, b, p]))
            loads.append((b, w_hbm.at[:, :, n], w.at[:, :, n], load_sem.at[1, b, p]))
    loads = [(b, pltpu.make_async_copy(x, y, z)) for b, x, y, z in loads]
    for _, copy in loads:
        copy.start()
    start_barrier()

    S_rows, R_rows = S.reshape(CHUNKS * 1024, LANES), R.reshape(CHUNKS * 1024, LANES)
    S2_rows, R2_rows = S2.reshape(CHUNKS * 1024, LANES), R2.reshape(CHUNKS * 1024, LANES)
    for b in range(CHUNKS):
        for at, copy in loads:
            if at == b:
                copy.wait()
        restrict_chunk(b, r, w, pat, A)
        pack_chunk(b, A, S_rows)
        if b == 0:
            end_barrier()
        send_chunk(S, R, b, s1, r1)
        keep_own(S, R, b)

    def couple(row, c):
        at = pl.ds(pl.multiple_of(row * 8, 8), 8)
        for d in range(4):
            there = opat[d, at, :].astype(F32)
            for e in range(9):
                coup[d * 9 + e, at, :] = off[d * 9 + e, at, :] * there
        return c

    lax.fori_loop(0, NI // 8, couple, 0)

    for b in range(CHUNKS):
        wait_chunk(R, b, r1)
        unfold_chunk(b, R_rows)
    gather_rows(slot, R_rows, G)
    cells_to_planes(G, odd, rhs)
    first_sweep(rhs, binv, X)
    for s in range(3):
        shift_columns(s, X, XL, XR, PL, PR)
        exchange_halo(s, X, PL, PR, HL, HR, hs, hr)
        fill_columns(s, XL, XR, HL, HR)
        sweep(s, rhs, binv, coup, X, XL, XR, (planes, rhs) if s == 2 else None)

    planes_to_cells(rhs, G)
    for b in range(CHUNKS):
        collect_chunk(b, inv, G, S2_rows)
        fold_chunk(b, S2_rows)
        send_chunk(S2, R2, b, s2, r2)
        keep_own(S2, R2, b)
    for b in range(CHUNKS):
        wait_chunk(R2, b, r2)
        spread_chunk(b, R2_rows, Y)

    for b in range(CHUNKS):
        wait_chunk(R, b, s1)
        wait_chunk(R, b, s2)
    for s in range(3):
        for sends, _, copy, _ in halo_copies(s, X, PL, PR, HL, HR, hs, hr):
            pl.when(sends)(copy.wait_send)


def prolong_kernel(y, w, pat, out):
    block = pl.program_id(0)
    del block

    def one(k, c):
        n = pl.multiple_of(k * LANES, LANES)
        base = pl.multiple_of(k * W, 8)
        there = bcast_row(pat, pl.ds(k, 1), slice(None)).astype(F32)
        src = [
            [y[pl.ds(base + i * 16 + qg * 8, 8), :] * there for qg in range(2)] for i in range(3)
        ]
        for j in range(3):
            acc = None
            for i in range(3):
                wij = jnp.broadcast_to(w[i, j : j + 1, pl.ds(n, LANES)], (8, LANES))
                terms = [wij * src[i][qg] for qg in range(2)]
                acc = terms if acc is None else [x + z for x, z in zip(acc, terms)]
            for qg in range(2):
                out[j, qg * 8 : qg * 8 + 8, pl.ds(n, LANES)] = acc[qg]
        return c

    lax.fori_loop(0, NK, one, 0)


def inverse_slots(owner, local):
    cell = jnp.arange(AGG, dtype=jnp.int32)
    by_owner = (owner[:, None] == jnp.arange(ND)[None]).astype(jnp.bfloat16)
    by_local = local[:, None] == jnp.arange(NK)[None]
    low = jnp.where(by_local, (cell % LANES)[:, None], 0).astype(jnp.bfloat16)
    high = jnp.where(by_local, (cell // LANES)[:, None], 0).astype(jnp.bfloat16)
    both = lax.dot_general(
        by_owner,
        jnp.concatenate([low, high], axis=1),
        (((0,), (0,)), ((), ())),
        preferred_element_type=F32,
    )
    found = (both[:, NK:] * LANES + both[:, :NK]).astype(jnp.int32)
    return found.reshape(ND, 3, 2, 4, 2).transpose(1, 0, 3, 2, 4).reshape(-1)


def body(residual, restriction, pattern, cell_aggregate, block_inverse, off_blocks, op_pattern):
    owner = (cell_aggregate // AGG).reshape(-1)
    local = (cell_aggregate % AGG // ND).reshape(-1)
    slot = (
        local // 16 * 1024 + owner * 8 + local % 8 // 2 * 2 + local // 8 % 2
    )
    odd = (local % 2).reshape(NI, LANES)
    inv = inverse_slots(owner, local)
    turned = residual.transpose(1, 0, 2)
    pat = pattern.reshape(384, LANES)

    vmem = pl.BlockSpec(memory_space=pltpu.VMEM)
    smem = pl.BlockSpec(memory_space=pltpu.SMEM)
    hbm = pl.BlockSpec(memory_space=pl.ANY)
    msg = pltpu.VMEM((CHUNKS, ND, 8, LANES), F32)
    plane = pltpu.VMEM((NI * W, LANES), F32)
    edge = pltpu.VMEM((3, W, LANES), F32)
    planes, y = pl.pallas_call(
        coarse_kernel,
        out_shape=(
            jax.ShapeDtypeStruct((NQ * 3 * NI, LANES), F32),
            jax.ShapeDtypeStruct((NK * W, LANES), F32),
        ),
        in_specs=[smem, smem, hbm, hbm, vmem, vmem, vmem, vmem, vmem],
        out_specs=(vmem, vmem),
        scratch_shapes=[
            pltpu.VMEM((3, NQ, FPA * AGG), F32),
            pltpu.VMEM((3, 3, FPA * AGG), F32),
            plane,
            msg,
            msg,
            msg,
            msg,
            pltpu.VMEM((AGG, LANES), F32),
            plane,
            pltpu.VMEM((3, (NI + 2) * W, LANES), F32),
            plane,
            plane,
            edge,
            edge,
            edge,
            edge,
            pltpu.VMEM((36, NI, LANES), F32),
            pltpu.SemaphoreType.DMA((2, CHUNKS, FPA)),
            pltpu.SemaphoreType.DMA((CHUNKS,)),
            pltpu.SemaphoreType.DMA((CHUNKS,)),
            pltpu.SemaphoreType.DMA((CHUNKS,)),
            pltpu.SemaphoreType.DMA((CHUNKS,)),
            pltpu.SemaphoreType.DMA((3, 4)),
            pltpu.SemaphoreType.DMA((3, 4)),
        ],
        compiler_params=pltpu.CompilerParams(
            collective_id=0, has_side_effects=True, vmem_limit_bytes=48 * 1024 * 1024
        ),
    )(
        slot,
        inv,
        turned,
        restriction,
        pat,
        odd,
        block_inverse.reshape(9, NI, LANES),
        off_blocks.reshape(36, NI, LANES),
        op_pattern,
    )
    fine = pl.pallas_call(
        prolong_kernel,
        grid=(FPA,),
        out_shape=jax.ShapeDtypeStruct((3, NQ, FPA * AGG), F32),
        in_specs=[
            pl.BlockSpec((NK * W, LANES), lambda p: (0, 0)),
            pl.BlockSpec((3, 3, AGG), lambda p: (0, 0, p)),
            pl.BlockSpec((NK, LANES), lambda p: (p, 0)),
        ],
        out_specs=pl.BlockSpec((3, NQ, AGG), lambda p: (0, 0, p)),
        compiler_params=pltpu.CompilerParams(vmem_limit_bytes=16 * 1024 * 1024),
    )(y, restriction, pat)
    return planes.reshape(NQ, 3, NI, LANES), fine.transpose(1, 0, 2)


def solution(mesh):
    in_specs = (
        P(None, None, ("row", "col")),
        P(None, None, ("row", "col")),
        P(("row", "col")),
        P("row", "col"),
        P(None, None, "row", "col"),
        P(None, None, None, "row", "col"),
        P(None, "row", "col"),
    )
    out_specs = (P(None, None, "row", "col"), P(None, None, ("row", "col")))
    return jax.shard_map(body, mesh=mesh, in_specs=in_specs, out_specs=out_specs, check_vma=False)
```

profile of v0, /device:TPU:1, one launch (start us, length us, event | category | flops | bytes accessed | tf_op | source)
XLA Modules:
  0.0 114.0 jit_solution(7955753724148657404)
XLA Ops:
  0.6 1.4 %fusion.10.slot = s32[6144]{0:T(1024)} fusion(s32[48,128]{1,0:T(8,128)} %param.10), kind=kLoop, calls=%fused_computation.42 | loop fusion | flops 540672 | bytes 49152 | tf_op jit(solution)/shard_map/add | solution.py:535
  2.1 1.4 %add_select_fusion = (s32[48,128]{1,0:T(8,128)}, s32[6144]{0:T(1024)S(1)}, s32[6144]{0:T(1024)S(1)}) fusion(s32[48,128]{1,0:T(8,128)} %param.10), kind=kLoop, calls=%fused_computation.9 | loop fusion | flops 233472 | bytes 98304 | tf_op jit(solution)/shard_map/jit(remainder)/select_n | solution.py:537
  3.5 0.2 select_convert_fusion.1
  3.7 0.0 copy-start.1
  3.7 1.1 fusion
  4.8 0.0 copy-start
  4.8 2.1 %copy.10 = s32[128,3,2,4,2]{4,2,3,0,1:T(2,128)} copy(s32[128,3,2,4,2]{0,4,3,2,1:T(2,128)S(1)} %bitcast.23) | data formatting | bytes 49152 | tf_op jit(solution)/shard_map/reshape | solution.py:528
  6.9 0.0 copy-start.4
  6.9 3.9 %reshape.56.inv = s32[6144]{0:T(1024)} reshape(s32[3,128,4,2,2]{4,3,2,1,0:T(2,128)} %bitcast.22) | data formatting | bytes 49152 | tf_op jit(solution)/shard_map/reshape | solution.py:528
  10.8 0.0 copy-done.1
  10.8 0.0 copy-done
  10.8 0.0 copy-done.2
  10.8 0.0 copy-done.4
  10.8 0.0 copy-start.3
  10.8 0.9 copy-done.3
  11.7 0.0 copy-start.5
  11.7 0.7 copy-done.5
  12.5 0.0 copy-start.6
  12.5 0.7 copy-done.6
  13.2 0.0 copy-start.7
  13.2 0.7 copy-done.7
  14.0 92.2 %shard_map.86 = (f32[2304,128]{1,0:T(8,128)S(1)}, f32[2304,128]{1,0:T(8,128)S(1)}) custom-call(s32[6144]{0:T(1024)S(1)} %copy-done.5, s32[6144]{0:T(1024)S(1)} %copy-done.7, f32[3,16,49152]{2,1,0:T(8,128)} %bitcast.20, f32[3,3,49152]{2,1,0:T(4,128)S(1)} %copy-done, s32[384,128]{1,0:T(8,128)S(1)} %bitcast.17, s32[48,128]{1,0:T(8,128)S(1)} %copy-done.6, ...), custom_call_target="tpu_custom_call" | custom-call | tf_op jit(solution)/shard_map/pallas_call | solution.py:548
  106.2 6.7 %shard_map.87 = f32[3,16,49152]{2,1,0:T(8,128)} custom-call(f32[2304,128]{1,0:T(8,128)S(1)} %get-tuple-element.5.y, f32[3,3,49152]{2,1,0:T(4,128)S(1)} %copy-done, s32[384,128]{1,0:T(8,128)S(1)} %bitcast.18), custom_call_target="tpu_custom_call" | custom-call | tf_op jit(solution)/shard_map/pallas_call | solution.py:596
  112.9 1.0 copy.12
  (3 shorter events, 0.0 us)
Async XLA Ops:
  3.7 7.1 %copy-start.1 = (f32[4,3,3,48,128]{4,3,2,1,0:T(8,128)S(1)}, f32[4,3,3,48,128]{4,3,2,1,0:T(8,128)}, u32[]{:S(2)}) copy-start(f32[4,3,3,48,128]{4,3,2,1,0:T(8,128)} %param.12) | copy-start | bytes 2654212
  4.8 6.0 %copy-start = (f32[3,3,49152]{2,1,0:T(4,128)S(1)}, f32[3,3,49152]{2,1,0:T(4,128)}, u32[]{:S(2)}) copy-start(f32[3,3,49152]{2,1,0:T(4,128)} %w.1) | copy-start | bytes 5308420
  6.9 3.9 %copy-start.2 = (s32[49152]{0:T(1024)S(1)}, s32[49152]{0:T(1024)}, u32[]{:S(2)}) copy-start(s32[49152]{0:T(1024)} %param.9) | copy-start | bytes 589828
  6.9 3.9 %copy-start.4 = (s32[4,48,128]{2,1,0:T(8,128)S(1)}, s32[4,48,128]{2,1,0:T(8,128)}, u32[]{:S(2)}) copy-start(s32[4,48,128]{2,1,0:T(8,128)} %opat.1) | copy-start | bytes 294916
  10.8 0.9 copy-start.3
  11.7 0.7 copy-start.5
  12.5 0.7 copy-start.6
  13.2 0.7 copy-start.7
where the time goes:
time: 114 us
  Pallas kernels  99 us (87%)
  local copies, waits for them, and re-layouts  10.2 us (9%)
  other arithmetic  3.05 us (3%)
    pallas_call x1, Pallas kernels, body(): pl.pallas_call(coarse_kernel, out_shape=(jax.ShapeDtypeStruct((NQ * 3 * N...  92.2 us
    pallas_call x1, Pallas kernels, body(): pl.pallas_call(prolong_kernel, grid=(FPA,), out_shape=jax.ShapeDtypeStruc...  6.74 us
    reshape x2, local copies, waits for them, and re-layouts, inverse_slots(): return found.reshape(ND, 3, 2, 4, 2).transpose(1, 0, 3, 2, 4).reshape(-1)  5.99 us
    unnamed x17, local copies, waits for them, and re-layouts  4.17 us

commit v1 on v0

v1 whole, which is shorter than its diff:
```python
import functools

import jax
import jax.numpy as jnp
from jax import lax
from jax.experimental import pallas as pl
from jax.experimental.pallas import tpu as pltpu
from jax.sharding import PartitionSpec as P

MESH = pl.DeviceIdType.MESH
ND = 128
NQ = 16
NI = 48
NK = 48
W = 48
AGG = 6144
FPA = 8
CHUNKS = 3
LANES = 128
F32 = jnp.float32


def me_index():
    return lax.axis_index("row") * 8 + lax.axis_index("col")


def lane_ids():
    return lax.broadcasted_iota(jnp.int32, (8, LANES), 1)


def bcast_row(ref, *idx):
    return jnp.broadcast_to(ref[idx], (8, LANES))


def each_peer(visit):
    row, col = lax.axis_index("row"), lax.axis_index("col")
    cols = [lax.rem(col + d, 8) for d in range(8)]
    for other in cols[1:]:
        visit(row, other)

    def one(d, c):
        there = lax.rem(row + d, 16)
        for other in cols:
            visit(there, other)
        return c

    lax.fori_loop(1, 16, one, 0)


def start_barrier():
    bar = pltpu.get_barrier_semaphore()
    each_peer(
        lambda row, col: pl.semaphore_signal(
            bar, inc=1, device_id=(row, col), device_id_type=MESH
        )
    )


def end_barrier():
    pl.semaphore_wait(pltpu.get_barrier_semaphore(), ND - 1)


def send_chunk(S, R, b, ssem, rsem):
    dst = R.at[b, me_index(), pl.ds(0, 6)]

    def visit(row, col):
        pltpu.make_async_remote_copy(
            S.at[b, row * 8 + col, pl.ds(0, 6)],
            dst,
            ssem.at[b],
            rsem.at[b],
            device_id=(row, col),
            device_id_type=MESH,
        ).start()

    each_peer(visit)


def wait_chunk(R, b, sem):
    block = R.at[b, pl.ds(0, ND - 1), pl.ds(0, 6)]
    pltpu.make_async_copy(block, block, sem.at[b]).wait()


def keep_own(S, R, b):
    me = me_index()
    R[b, me] = S[b, me]


def restrict_chunk(b, r, w, pat, A):
    def one(kk, c):
        k = b * 16 + kk
        acc = [[None] * 2 for _ in range(3)]
        for p in range(FPA):
            n = pl.multiple_of(p * AGG + k * LANES, LANES)
            there = bcast_row(pat, pl.ds(p * 48 + k, 1), slice(None)).astype(F32)
            here = [
                [r[j, qg * 8 : qg * 8 + 8, pl.ds(n, LANES)] * there for qg in range(2)]
                for j in range(3)
            ]
            for i in range(3):
                for j in range(3):
                    wij = jnp.broadcast_to(w[i, j : j + 1, pl.ds(n, LANES)], (8, LANES))
                    for qg in range(2):
                        term = wij * here[j][qg]
                        acc[i][qg] = term if acc[i][qg] is None else acc[i][qg] + term
        for i in range(3):
            for qg in range(2):
                at = pl.multiple_of(k * W + i * 16 + qg * 8, 8)
                A[pl.ds(at, 8), :] = acc[i][qg]
        return c

    lax.fori_loop(0, 16, one, 0)


def pack_chunk(b, A, S2d):
    for h in range(2):
        k8 = b * 16 + 8 * h
        six, seven = (k8 + 6) * W, (k8 + 7) * W
        for m in range(3):
            at = (k8 + 2 * m) * W
            head = A[at : at + 96, :]
            if m == 0:
                tail = [A[six : six + 32, :]]
            elif m == 1:
                tail = [A[seven : seven + 32, :]]
            else:
                tail = [A[six + 32 : six + 48, :], A[seven + 32 : seven + 48, :]]
            turned = jnp.concatenate([head] + tail, axis=0).T
            for t0 in range(16):
                rows = pl.ds(b * 1024 + t0 * 64 + 2 * m + h, 8, stride=8)
                S2d[rows, :] = turned[t0 * 8 : t0 * 8 + 8, :]


def unfold_chunk(b, R2d):
    lane = lane_ids()

    def one(fb, c):
        for base, h in [(b * 1024 + (fb * 4 + u) * 64, h) for u in range(4) for h in range(2)]:
            x0 = R2d[pl.ds(base + h, 8, stride=8), :]
            x1 = R2d[pl.ds(base + 2 + h, 8, stride=8), :]
            x2 = R2d[pl.ds(base + 4 + h, 8, stride=8), :]
            six = jnp.where(lane < 32, pltpu.roll(x0, 32, 1), pltpu.roll(x2, 64, 1))
            seven = jnp.where(lane < 80, pltpu.roll(x1, 80, 1), pltpu.roll(x2, 96, 1))
            R2d[pl.ds(base + 6 + h, 8, stride=8), :] = jnp.where(lane < 48, six, seven)
        return c

    lax.fori_loop(0, 4, one, 0)


def fold_chunk(b, S2d):
    lane = lane_ids()

    def one(fb, c):
        for base, h in [(b * 1024 + (fb * 4 + u) * 64, h) for u in range(4) for h in range(2)]:
            d = S2d[pl.ds(base + 6 + h, 8, stride=8), :]
            late = lane >= 96
            for m, moved in enumerate(
                (
                    pltpu.roll(d, 96, 1),
                    pltpu.roll(d, 48, 1),
                    jnp.where(lane < 112, pltpu.roll(d, 64, 1), pltpu.roll(d, 32, 1)),
                )
            ):
                rows = pl.ds(base + 2 * m + h, 8, stride=8)
                S2d[rows, :] = jnp.where(late, moved, S2d[rows, :])
        return c

    lax.fori_loop(0, 4, one, 0)


def index_tables(ca, slot_v, odd, inv_v):
    def one(blk, acc):
        rows = pl.ds(pl.multiple_of(blk * 8, 8), 8)
        pair = lax.shift_right_logical(ca[rows, :], 7)
        owner = lax.shift_right_logical(lax.shift_right_logical(pair, 4) * 171, 9)
        local = pair - owner * NK
        bit = [lax.shift_right_logical(local, n) & 1 for n in range(4)]
        chunk = lax.shift_right_logical(local, 4)
        at = chunk * 1024 + owner * 8 + (bit[2] * 2 + bit[1]) * 2 + bit[3]
        slot_v[rows, :] = jnp.clip(at, 0, CHUNKS * 1024 - 1)
        odd[rows, :] = bit[0]
        for u in range(8):
            who = jnp.broadcast_to(owner[u : u + 1], (ND, LANES))
            by_owner = (who == lax.broadcasted_iota(jnp.int32, (ND, LANES), 0)).astype(F32)
            which = jnp.broadcast_to(local[u : u + 1], (NK, LANES))
            here = which == lax.broadcasted_iota(jnp.int32, (NK, LANES), 0)
            column = lax.broadcasted_iota(jnp.int32, (NK, LANES), 1).astype(F32)
            line = (blk * 8 + u).astype(F32)
            cells = jnp.concatenate(
                [jnp.where(here, column, 0.0), jnp.where(here, line, 0.0)], axis=0
            )
            acc = acc + lax.dot_general(
                by_owner.astype(jnp.bfloat16),
                cells.astype(jnp.bfloat16),
                (((1,), (1,)), ((), ())),
                preferred_element_type=F32,
            )
        return acc

    acc = lax.fori_loop(0, NI // 8, one, jnp.zeros((ND, 2 * NK), F32))
    cell = (acc[:, NK:] * LANES + acc[:, :NK]).astype(jnp.int32)
    inv_v[:, 0:NK] = jnp.clip(cell, 0, AGG - 1)


def gather_rows(slot, R2d, G):
    def some(row, c):
        base = pl.multiple_of(row * LANES, LANES)
        for u in range(LANES):
            G[pl.ds(base + u, 1), :] = R2d[pl.ds(slot[row, u], 1), :]
        return c

    lax.fori_loop(0, NI, some, 0)


def solve_block(binv, row, total):
    out = []
    for i in range(3):
        acc = None
        for j in range(3):
            coef = bcast_row(binv, i * 3 + j, pl.ds(row, 1), slice(None))
            terms = [coef * total[j][qg] for qg in range(2)]
            acc = terms if acc is None else [x + y for x, y in zip(acc, terms)]
        out.append(acc)
    return out


def cells_to_planes(G, odd, rhs, binv, X):
    def one(two, c):
        for u in range(4):
            row = two * 4 + u
            base = pl.multiple_of(row * W, 8)
            turned = G[pl.ds(pl.multiple_of(row * LANES, LANES), LANES), :].T
            is_odd = bcast_row(odd, pl.ds(row, 1), slice(None)) == 1
            total = [[None] * 2 for _ in range(3)]
            for v in range(6):
                here = jnp.where(
                    is_odd, turned[W + v * 8 : W + v * 8 + 8, :], turned[v * 8 : v * 8 + 8, :]
                )
                rhs[pl.ds(base + v * 8, 8), :] = here
                total[v // 2][v % 2] = here
            new = solve_block(binv, row, total)
            for v in range(6):
                X[0, pl.ds(base + W + v * 8, 8), :] = new[v // 2][v % 2]
        return c

    lax.fori_loop(0, NI // 4, one, 0)


def couplings(off, opat, binv, coup, pc, pb):
    def couple(blk, c):
        at = pl.ds(pl.multiple_of(blk * 8, 8), 8)
        for d in range(4):
            there = opat[d, at, :].astype(F32)
            for e in range(9):
                coup[d * 9 + e, at, :] = off[d * 9 + e, at, :] * there
        return c

    lax.fori_loop(0, NI // 8, couple, 0)

    def pack(e, c):
        for blk in range(3):
            for src, plane, keep in (
                (coup, 18 + e, (0,)),
                (coup, 27 + e, (1,)),
                (binv, e, (0, 1)),
            ):
                parts = [
                    bcast_row(src, plane, slice(blk * 16 + n, blk * 16 + n + 1), slice(None))
                    for n in range(16)
                ]
                turned = jnp.concatenate(parts, axis=0).T
                for side in keep:
                    line = turned[0:1] if side == 0 else turned[LANES - 1 : LANES]
                    dst = pb if src is binv else pc
                    for qg in range(2):
                        dst[side, e, qg * 3 + blk : qg * 3 + blk + 1, :] = line
        return c

    lax.fori_loop(0, 9, pack, 0)

    def mask(e, c):
        lane = lax.broadcasted_iota(jnp.int32, (NI, LANES), 1)
        coup[18 + e] = jnp.where(lane == 0, 0.0, coup[18 + e])
        coup[27 + e] = jnp.where(lane == LANES - 1, 0.0, coup[27 + e])
        return c

    lax.fori_loop(0, 9, mask, 0)


def pack_edges(s, X, E):
    for blk in range(3):
        for v in range(6):
            parts = [
                X[s, (blk * 16 + n + 1) * W + v * 8 : (blk * 16 + n + 1) * W + v * 8 + 8, :]
                for n in range(16)
            ]
            turned = jnp.concatenate(parts, axis=0).T
            at = v % 2 * 3 + blk
            E[0, s, v // 2, at : at + 1, :] = turned[0:1]
            E[1, s, v // 2, at : at + 1, :] = turned[LANES - 1 : LANES]


def halo_copies(s, X, E, H, hs, hr):
    row, col = lax.axis_index("row"), lax.axis_index("col")
    own_first = X.at[s, pl.ds(W, W)]
    own_last = X.at[s, pl.ds(NI * W, W)]
    above = X.at[s, pl.ds(0, W)]
    below = X.at[s, pl.ds((NI + 1) * W, W)]
    table = [
        (row > 0, row < 15, own_first, below, (row - 1, col)),
        (row < 15, row > 0, own_last, above, (row + 1, col)),
        (col > 0, col < 7, E.at[0, s], H.at[1, s], (row, col - 1)),
        (col < 7, col > 0, E.at[1, s], H.at[0, s], (row, col + 1)),
    ]
    return [
        (
            sends,
            receives,
            pltpu.make_async_remote_copy(
                src, dst, hs.at[s, n], hr.at[s, n], device_id=dev, device_id_type=MESH
            ),
            dst,
        )
        for n, (sends, receives, src, dst, dev) in enumerate(table)
    ]


def start_copies(copies):
    for sends, _, copy, _ in copies:
        pl.when(sends)(copy.start)


def finish_copies(copies):
    for _, receives, copy, dst in copies:
        pl.when(receives)(copy.wait_recv)

        def clear(dst=dst):
            dst[...] = jnp.zeros(dst.shape, F32)

        pl.when(jnp.logical_not(receives))(clear)


def sweep_row(s, row, rhs, binv, coup, X, new_at):
    base = pl.multiple_of(row * W, 8)

    def at(v):
        return pl.ds(base + v * 8, 8)

    own = [X[s, at(v + 6), :] for v in range(6)]
    left = [pltpu.roll(x, 1, 1) for x in own]
    right = [pltpu.roll(x, LANES - 1, 1) for x in own]
    total = [[rhs[at(j * 2 + qg), :] for qg in range(2)] for j in range(3)]
    for d in range(4):
        for k in range(3):
            near = []
            for qg in range(2):
                v = k * 2 + qg
                if d == 0:
                    near.append(X[s, at(v), :])
                elif d == 1:
                    near.append(X[s, at(v + 12), :])
                else:
                    near.append((left if d == 2 else right)[v])
            for j in range(3):
                coef = bcast_row(coup, d * 9 + j * 3 + k, pl.ds(row, 1), slice(None))
                for qg in range(2):
                    total[j][qg] = total[j][qg] - coef * near[qg]
    new = solve_block(binv, row, total)
    for v in range(6):
        new_at(row, v)[...] = new[v // 2][v % 2]


def correct_edges(s, H, pc, pb, D):
    for side in range(2):
        push = []
        for j in range(3):
            acc = None
            for k in range(3):
                term = pc[side, j * 3 + k] * H[side, s, k]
                acc = term if acc is None else acc + term
            push.append(acc)
        for i in range(3):
            acc = None
            for j in range(3):
                term = pb[side, i * 3 + j] * push[j]
                acc = term if acc is None else acc + term
            D[side, i] = -acc


def add_edges(blk, D, new_at):
    sub = lax.broadcasted_iota(jnp.int32, (8, LANES), 0)
    zero = jnp.zeros((LANES - 16, LANES), F32)
    for v in range(6):
        at = v % 2 * 3 + blk
        first = jnp.where(sub == 0, bcast_row(D, 0, v // 2, slice(at, at + 1), slice(None)), 0.0)
        last = jnp.where(sub == 7, bcast_row(D, 1, v // 2, slice(at, at + 1), slice(None)), 0.0)
        turned = jnp.concatenate([first, zero, last], axis=0).T
        for n in range(16):
            ref = new_at(blk * 16 + n, v)
            ref[...] = ref[...] + turned[n * 8 : n * 8 + 8]


def planes_to_cells(last, G):
    def one(blk, c):
        for u in range(4):
            row = blk * 4 + u
            x = last[pl.ds(pl.multiple_of(row * W, 8), W), :]
            turned = jnp.concatenate([x, x, x[0:32]], axis=0).T
            G[pl.ds(pl.multiple_of(row * LANES, LANES), LANES), :] = turned
        return c

    lax.fori_loop(0, NI // 4, one, 0)


def collect_chunk(b, inv, G, S2d):
    lane = lax.broadcasted_iota(jnp.int32, (1, LANES), 1)

    def one(fb, c):
        for u in range(4):
            f = fb * 4 + u
            for rr in range(8):
                k = b * 16 + rr % 2 * 8 + rr // 2 * 2
                even = G[pl.ds(inv[f, k], 1), :]
                odd = G[pl.ds(inv[f, k + 1], 1), :]
                S2d[pl.ds(b * 1024 + f * 8 + rr, 1), :] = jnp.where(lane < W, even, odd)
        return c

    lax.fori_loop(0, ND // 4, one, 0)


def spread_chunk(b, R2d, Y):
    for h in range(2):
        k8 = b * 16 + 8 * h
        six, seven = (k8 + 6) * W, (k8 + 7) * W
        for m in range(3):
            parts = [
                R2d[pl.ds(b * 1024 + t0 * 64 + 2 * m + h, 8, stride=8), :] for t0 in range(16)
            ]
            turned = jnp.concatenate(parts, axis=0).T
            at = (k8 + 2 * m) * W
            Y[at : at + 96, :] = turned[0:96]
            if m == 0:
                Y[six : six + 32, :] = turned[96:128]
            elif m == 1:
                Y[seven : seven + 32, :] = turned[96:128]
            else:
                Y[six + 32 : six + 48, :] = turned[96:112]
                Y[seven + 32 : seven + 48, :] = turned[112:128]


def coarse_kernel(
    r_hbm,
    w_hbm,
    pat_hbm,
    ca_hbm,
    binv_hbm,
    off_hbm,
    opat_hbm,
    x_out,
    Y,
    r,
    w,
    pat,
    ca,
    binv,
    off,
    opat,
    A,
    S,
    R,
    S2,
    R2,
    G,
    rhs,
    X,
    E,
    H,
    D,
    coup,
    pc,
    pb,
    slot_v,
    odd,
    inv_v,
    slot,
    inv,
    load_sem,
    small_sem,
    s1,
    r1,
    s2,
    r2,
    hs,
    hr,
):
    small = [
        pltpu.make_async_copy(x, y, small_sem.at[n])
        for n, (x, y) in enumerate(
            [
                (pat_hbm, pat),
                (ca_hbm, ca),
                (binv_hbm, binv),
                (off_hbm, off),
                (opat_hbm, opat),
                (slot_v, slot),
                (inv_v, inv),
            ]
        )
    ]
    loads = []
    for b in range(CHUNKS):
        for p in range(FPA):
            n = pl.ds(p * AGG + b * 2048, 2048)
            loads.append((b, r_hbm.at[:, :, n], r.at[:, :, n], load_sem.at[0, b, p]))
            loads.append((b, w_hbm.at[:, :, n], w.at[:, :, n], load_sem.at[1, b, p]))
    loads = [(b, pltpu.make_async_copy(x, y, z)) for b, x, y, z in loads]
    small[0].start()
    for _, copy in loads:
        copy.start()
    for copy in small[1:5]:
        copy.start()
    start_barrier()

    S_rows, R_rows = S.reshape(CHUNKS * 1024, LANES), R.reshape(CHUNKS * 1024, LANES)
    S2_rows, R2_rows = S2.reshape(CHUNKS * 1024, LANES), R2.reshape(CHUNKS * 1024, LANES)
    small[0].wait()
    for b in range(CHUNKS):
        for at, copy in loads:
            if at == b:
                copy.wait()
        restrict_chunk(b, r, w, pat, A)
        pack_chunk(b, A, S_rows)
        if b == 0:
            end_barrier()
        send_chunk(S, R, b, s1, r1)
        keep_own(S, R, b)

    for copy in small[1:5]:
        copy.wait()
    E[...] = jnp.zeros(E.shape, F32)
    pc[...] = jnp.zeros(pc.shape, F32)
    pb[...] = jnp.zeros(pb.shape, F32)
    inv_v[...] = jnp.zeros(inv_v.shape, jnp.int32)
    index_tables(ca, slot_v, odd, inv_v)
    small[5].start()
    small[6].start()
    couplings(off, opat, binv, coup, pc, pb)
    small[5].wait()
    small[6].wait()

    for b in range(CHUNKS):
        wait_chunk(R, b, r1)
        unfold_chunk(b, R_rows)
    gather_rows(slot, R_rows, G)
    cells_to_planes(G, odd, rhs, binv, X)

    halos = [halo_copies(s, X, E, H, hs, hr) for s in range(3)]
    start_copies(halos[0][:2])
    pack_edges(0, X, E)
    start_copies(halos[0][2:])
    for s in range(3):
        if s < 2:

            def new_at(row, v, s=s):
                return X.at[s + 1, pl.ds(pl.multiple_of(row * W + W + v * 8, 8), 8)]
        else:

            def new_at(row, v):
                return x_out.at[pl.ds(pl.multiple_of(row * W + v * 8, 8), 8)]

        def inner(two, c, s=s, new_at=new_at):
            for u in range(2):
                sweep_row(s, 1 + two * 2 + u, rhs, binv, coup, X, new_at)
            return c

        lax.fori_loop(0, (NI - 2) // 2, inner, 0)
        finish_copies(halos[s][:2])
        lax.fori_loop(
            0,
            2,
            lambda n, c, s=s, new_at=new_at: (
                sweep_row(s, n * (NI - 1), rhs, binv, coup, X, new_at),
                c,
            )[1],
            0,
        )
        finish_copies(halos[s][2:])
        correct_edges(s, H, pc, pb, D)
        add_edges(0, D, new_at)
        add_edges(2, D, new_at)
        if s < 2:
            start_copies(halos[s + 1][:2])
        add_edges(1, D, new_at)
        if s < 2:
            pack_edges(s + 1, X, E)
            start_copies(halos[s + 1][2:])

    planes_to_cells(x_out, G)
    for b in range(CHUNKS):
        collect_chunk(b, inv, G, S2_rows)
        fold_chunk(b, S2_rows)
        send_chunk(S2, R2, b, s2, r2)
        keep_own(S2, R2, b)
    for b in range(CHUNKS):
        wait_chunk(R2, b, r2)
        spread_chunk(b, R2_rows, Y)

    for b in range(CHUNKS):
        wait_chunk(R, b, s1)
        wait_chunk(R, b, s2)
    for copies in halos:
        for sends, _, copy, _ in copies:
            pl.when(sends)(copy.wait_send)


def prolong_kernel(y, x, w, pat, out, planes):
    step = pl.program_id(0)

    def line(n, c):
        row = step * 6 + n
        for v in range(6):
            at = (v % 2 * 24 + v // 2) * NI + row
            planes[pl.ds(at, 8, stride=3 * NI), :] = x[pl.ds(row * W + v * 8, 8), :]
        return c

    lax.fori_loop(0, NI // FPA, line, 0)

    def one(k, c):
        n = pl.multiple_of(k * LANES, LANES)
        base = pl.multiple_of(k * W, 8)
        there = bcast_row(pat, pl.ds(k, 1), slice(None)).astype(F32)
        src = [
            [y[pl.ds(base + i * 16 + qg * 8, 8), :] * there for qg in range(2)] for i in range(3)
        ]
        for j in range(3):
            acc = None
            for i in range(3):
                wij = jnp.broadcast_to(w[i, j : j + 1, pl.ds(n, LANES)], (8, LANES))
                terms = [wij * src[i][qg] for qg in range(2)]
                acc = terms if acc is None else [x + z for x, z in zip(acc, terms)]
            for qg in range(2):
                out[j, qg * 8 : qg * 8 + 8, pl.ds(n, LANES)] = acc[qg]
        return c

    lax.fori_loop(0, NK, one, 0)


def body(residual, restriction, pattern, cell_aggregate, block_inverse, off_blocks, op_pattern):
    turned = residual.transpose(1, 0, 2)
    pat = pattern.reshape(384, LANES)
    vmem = pl.BlockSpec(memory_space=pltpu.VMEM)
    hbm = pl.BlockSpec(memory_space=pltpu.HBM)
    msg = pltpu.VMEM((CHUNKS, ND, 8, LANES), F32)
    plane = pltpu.VMEM((NI * W, LANES), F32)
    edge = pltpu.VMEM((2, 3, 3, 8, LANES), F32)
    x, y = pl.pallas_call(
        coarse_kernel,
        out_shape=(
            jax.ShapeDtypeStruct((NI * W, LANES), F32),
            jax.ShapeDtypeStruct((NK * W, LANES), F32),
        ),
        in_specs=[hbm] * 7,
        out_specs=(vmem, vmem),
        scratch_shapes=[
            pltpu.VMEM((3, NQ, FPA * AGG), F32),
            pltpu.VMEM((3, 3, FPA * AGG), F32),
            pltpu.VMEM((384, LANES), jnp.int32),
            pltpu.VMEM((NI, LANES), jnp.int32),
            pltpu.VMEM((9, NI, LANES), F32),
            pltpu.VMEM((36, NI, LANES), F32),
            pltpu.VMEM((4, NI, LANES), jnp.int32),
            plane,
            msg,
            msg,
            msg,
            msg,
            pltpu.VMEM((AGG, LANES), F32),
            plane,
            pltpu.VMEM((3, (NI + 2) * W, LANES), F32),
            edge,
            edge,
            pltpu.VMEM((2, 3, 8, LANES), F32),
            pltpu.VMEM((36, NI, LANES), F32),
            pltpu.VMEM((2, 9, 8, LANES), F32),
            pltpu.VMEM((2, 9, 8, LANES), F32),
            pltpu.VMEM((NI, LANES), jnp.int32),
            pltpu.VMEM((NI, LANES), jnp.int32),
            pltpu.VMEM((ND, LANES), jnp.int32),
            pltpu.SMEM((NI, LANES), jnp.int32),
            pltpu.SMEM((ND, LANES), jnp.int32),
            pltpu.SemaphoreType.DMA((2, CHUNKS, FPA)),
            pltpu.SemaphoreType.DMA((7,)),
            pltpu.SemaphoreType.DMA((CHUNKS,)),
            pltpu.SemaphoreType.DMA((CHUNKS,)),
            pltpu.SemaphoreType.DMA((CHUNKS,)),
            pltpu.SemaphoreType.DMA((CHUNKS,)),
            pltpu.SemaphoreType.DMA((3, 4)),
            pltpu.SemaphoreType.DMA((3, 4)),
        ],
        compiler_params=pltpu.CompilerParams(
            collective_id=0, has_side_effects=True, vmem_limit_bytes=46 * 1024 * 1024
        ),
    )(
        *[
            pltpu.with_memory_space_constraint(x, pltpu.HBM)
            for x in (
                turned,
                restriction,
                pat,
                cell_aggregate,
                block_inverse.reshape(9, NI, LANES),
                off_blocks.reshape(36, NI, LANES),
                op_pattern,
            )
        ]
    )
    fine, planes = pl.pallas_call(
        prolong_kernel,
        grid=(FPA,),
        out_shape=(
            jax.ShapeDtypeStruct((3, NQ, FPA * AGG), F32),
            jax.ShapeDtypeStruct((NQ * 3 * NI, LANES), F32),
        ),
        in_specs=[
            vmem,
            vmem,
            pl.BlockSpec((3, 3, AGG), lambda p: (0, 0, p)),
            pl.BlockSpec((NK, LANES), lambda p: (p, 0)),
        ],
        out_specs=(
            pl.BlockSpec((3, NQ, AGG), lambda p: (0, 0, p)),
            pl.BlockSpec((NQ * 3 * NI, LANES), lambda p: (0, 0)),
        ),
        compiler_params=pltpu.CompilerParams(vmem_limit_bytes=16 * 1024 * 1024),
    )(y, x, restriction, pat)
    return planes.reshape(NQ, 3, NI, LANES), fine.transpose(1, 0, 2)


def solution(mesh):
    in_specs = (
        P(None, None, ("row", "col")),
        P(None, None, ("row", "col")),
        P(("row", "col")),
        P("row", "col"),
        P(None, None, "row", "col"),
        P(None, None, None, "row", "col"),
        P(None, "row", "col"),
    )
    out_specs = (P(None, None, "row", "col"), P(None, None, ("row", "col")))
    return jax.shard_map(body, mesh=mesh, in_specs=in_specs, out_specs=out_specs, check_vma=False)
```

time: 114 us -> 77.8 us (0.68)
  Pallas kernels: 99 us -> 77 us
  local copies, waits for them, and re-layouts: 10.2 us -> 0.01 us
  other arithmetic: 3.05 us -> 0 us
    pallas_call x2, Pallas kernels: 99 us -> 77 us  [the longest x1 68.9 us: body(): pl.pallas_call(coarse_kernel, out_shape=(jax.ShapeDtypeStruct((NI * W, LA...]
    reshape x2 -> x0, local copies, waits for them, and re-layouts: 5.99 us -> none  [inverse_slots(): return found.reshape(ND, 3, 2, 4, 2).transpose(1, 0, 3, 2, 4).reshape(-1)]
    unnamed x17 -> x4, local copies, waits for them, and re-layouts: 4.17 us -> 0.01 us
    add x1 -> x0, other arithmetic: 1.45 us -> none  [body(): slot = local // 16 * 1024 + owner * 8 + local % 8 // 2 * 2 + local // 8 % 2]
    select_n x2 -> x0, other arithmetic: 1.4 us -> none  [the longest x1 1.39 us: body(): odd = (local % 2).reshape(NI, LANES)]
where the time goes in v1:
time: 77.8 us; the launch traced here: 77.7 us
  Pallas kernels  77 us (99%)
    pallas_call x1, Pallas kernels, body(): pl.pallas_call(coarse_kernel, out_shape=(jax.ShapeDtypeStruct((NI * W, LA...  68.9 us
    pallas_call x1, Pallas kernels, body(): pl.pallas_call(prolong_kernel, grid=(FPA,), out_shape=(jax.ShapeDtypeStru...  8.11 us

profile of v1, /device:TPU:1, one launch (start us, length us, event | category | flops | bytes accessed | tf_op | source)
XLA Modules:
  0.0 77.7 jit_solution(12389567088167283628)
XLA Ops:
  0.6 0.0 copy-start
  0.6 0.0 copy-start.1
  0.7 68.9 %shard_map.86 = (f32[2304,128]{1,0:T(8,128)S(1)}, f32[2304,128]{1,0:T(8,128)S(1)}) custom-call(f32[3,16,49152]{2,1,0:T(8,128)} %bitcast.8, f32[3,3,49152]{2,1,0:T(4,128)} %w.1, s32[384,128]{1,0:T(8,128)} %bitcast.6, s32[48,128]{1,0:T(8,128)} %ca_hbm.1, f32[9,48,128]{2,1,0:T(8,128)} %bitcast.10, f32[36,48,128]{2,1,0:T(8,128)} %bitcast.9, s32[4,48,128]{2,1,0:T(8,128)} %opat_hbm.1), custom_call_target="tpu_custom_call" | custom-call | tf_op jit(solution)/shard_map/pallas_call | solution.py:656
  69.6 0.0 copy-done
  69.6 0.0 copy-done.1
  69.6 8.1 %shard_map.87 = (f32[3,16,49152]{2,1,0:T(8,128)}, f32[2304,128]{1,0:T(8,128)}) custom-call(f32[2304,128]{1,0:T(8,128)S(1)} %get-tuple-element.6.y, f32[2304,128]{1,0:T(8,128)S(1)} %get-tuple-element.7.x, f32[3,3,49152]{2,1,0:T(4,128)S(1)} %copy-done, s32[384,128]{1,0:T(8,128)S(1)} %bitcast.7), custom_call_target="tpu_custom_call" | custom-call | tf_op jit(solution)/shard_map/pallas_call | solution.py:717
Async XLA Ops:
  0.6 68.9 %copy-start = (f32[3,3,49152]{2,1,0:T(4,128)S(1)}, f32[3,3,49152]{2,1,0:T(4,128)}, u32[]{:S(2)}) copy-start(f32[3,3,49152]{2,1,0:T(4,128)} %w.1) | copy-start | bytes 5308420
  0.6 68.9 %copy-start.1 = (s32[49152]{0:T(1024)S(1)}, s32[49152]{0:T(1024)}, u32[]{:S(2)}) copy-start(s32[49152]{0:T(1024)} %param.9) | copy-start | bytes 589828

commit v2 on v1

--- a/solution.py
+++ b/solution.py
@@ -142,27 +142,6 @@
             six = jnp.where(lane < 32, pltpu.roll(x0, 32, 1), pltpu.roll(x2, 64, 1))
             seven = jnp.where(lane < 80, pltpu.roll(x1, 80, 1), pltpu.roll(x2, 96, 1))
             R2d[pl.ds(base + 6 + h, 8, stride=8), :] = jnp.where(lane < 48, six, seven)
-        return c
-
-    lax.fori_loop(0, 4, one, 0)
-
-
-def fold_chunk(b, S2d):
-    lane = lane_ids()
-
-    def one(fb, c):
-        for base, h in [(b * 1024 + (fb * 4 + u) * 64, h) for u in range(4) for h in range(2)]:
-            d = S2d[pl.ds(base + 6 + h, 8, stride=8), :]
-            late = lane >= 96
-            for m, moved in enumerate(
-                (
-                    pltpu.roll(d, 96, 1),
-                    pltpu.roll(d, 48, 1),
-                    jnp.where(lane < 112, pltpu.roll(d, 64, 1), pltpu.roll(d, 32, 1)),
-                )
-            ):
-                rows = pl.ds(base + 2 * m + h, 8, stride=8)
-                S2d[rows, :] = jnp.where(late, moved, S2d[rows, :])
         return c
 
     lax.fori_loop(0, 4, one, 0)
@@ -225,9 +204,9 @@
 
 
 def cells_to_planes(G, odd, rhs, binv, X):
-    def one(two, c):
-        for u in range(4):
-            row = two * 4 + u
+    def one(blk, c):
+        for u in range(8):
+            row = blk * 8 + u
             base = pl.multiple_of(row * W, 8)
             turned = G[pl.ds(pl.multiple_of(row * LANES, LANES), LANES), :].T
             is_odd = bcast_row(odd, pl.ds(row, 1), slice(None)) == 1
@@ -243,7 +222,7 @@
                 X[0, pl.ds(base + W + v * 8, 8), :] = new[v // 2][v % 2]
         return c
 
-    lax.fori_loop(0, NI // 4, one, 0)
+    lax.fori_loop(0, NI // 8, one, 0)
 
 
 def couplings(off, opat, binv, coup, pc, pb):
@@ -402,30 +381,90 @@
 
 def planes_to_cells(last, G):
     def one(blk, c):
-        for u in range(4):
-            row = blk * 4 + u
+        for u in range(8):
+            row = blk * 8 + u
             x = last[pl.ds(pl.multiple_of(row * W, 8), W), :]
-            turned = jnp.concatenate([x, x, x[0:32]], axis=0).T
-            G[pl.ds(pl.multiple_of(row * LANES, LANES), LANES), :] = turned
-        return c
-
-    lax.fori_loop(0, NI // 4, one, 0)
-
-
-def collect_chunk(b, inv, G, S2d):
-    lane = lax.broadcasted_iota(jnp.int32, (1, LANES), 1)
-
-    def one(fb, c):
-        for u in range(4):
-            f = fb * 4 + u
+            turned = jnp.concatenate([x, x], axis=0).T
+            G[pl.ds(pl.multiple_of(row * LANES, LANES), LANES), 0 : 2 * W] = turned
+        return c
+
+    lax.fori_loop(0, NI // 8, one, 0)
+
+
+def return_all(inv, G, S2, S2_rows, R2, ssem, rsem):
+    row, col = lax.axis_index("row"), lax.axis_index("col")
+    cols = [lax.rem(col + d, 8) for d in range(8)]
+    me = me_index()
+    low = lax.broadcasted_iota(jnp.int32, (1, LANES), 1) < W
+    lane = lane_ids()
+
+    def collect(b, there):
+        for u in range(8):
+            f = there * 8 + u
             for rr in range(8):
                 k = b * 16 + rr % 2 * 8 + rr // 2 * 2
                 even = G[pl.ds(inv[f, k], 1), :]
                 odd = G[pl.ds(inv[f, k + 1], 1), :]
-                S2d[pl.ds(b * 1024 + f * 8 + rr, 1), :] = jnp.where(lane < W, even, odd)
-        return c
-
-    lax.fori_loop(0, ND // 4, one, 0)
+                S2_rows[pl.ds(b * 1024 + f * 8 + rr, 1), :] = jnp.where(low, even, odd)
+
+    def fold_start(b, there):
+        base = b * 1024 + there * 64
+        done = []
+        for h in range(2):
+            d = S2_rows[pl.ds(base + 6 + h, 8, stride=8), :]
+            for m, moved in enumerate(
+                (
+                    pltpu.roll(d, 96, 1),
+                    pltpu.roll(d, 48, 1),
+                    jnp.where(lane < 112, pltpu.roll(d, 64, 1), pltpu.roll(d, 32, 1)),
+                )
+            ):
+                rows = pl.ds(base + 2 * m + h, 8, stride=8)
+                done.append((rows, jnp.where(lane >= 96, moved, S2_rows[rows, :])))
+        return done
+
+    def fold_end(done):
+        for rows, x in done:
+            S2_rows[rows, :] = x
+
+    def send(b, there):
+        def one(c):
+            pltpu.make_async_remote_copy(
+                S2.at[b, there * 8 + c, pl.ds(0, 6)],
+                R2.at[b, me, pl.ds(0, 6)],
+                ssem.at[b],
+                rsem.at[b],
+                device_id=(there, c),
+                device_id_type=MESH,
+            ).start()
+
+        for c in cols[1:]:
+            one(c)
+        pl.when(there != row)(lambda: one(cols[0]))
+
+    def peer(d):
+        return lax.rem(row + d, 16)
+
+    for b in range(CHUNKS):
+        collect(b, peer(0))
+        done = fold_start(b, peer(0))
+        if b > 0:
+            send(b - 1, peer(15))
+        collect(b, peer(1))
+        fold_end(done)
+
+        def step(d, c, b=b):
+            done = fold_start(b, peer(d - 1))
+            collect(b, peer(d))
+            fold_end(done)
+            send(b, peer(d - 2))
+            return c
+
+        lax.fori_loop(2, 16, step, 0)
+        fold_end(fold_start(b, peer(15)))
+        send(b, peer(14))
+        R2[b, me] = S2[b, me]
+    send(CHUNKS - 1, peer(15))
 
 
 def spread_chunk(b, R2d, Y):
@@ -514,12 +553,15 @@
             loads.append((b, r_hbm.at[:, :, n], r.at[:, :, n], load_sem.at[0, b, p]))
             loads.append((b, w_hbm.at[:, :, n], w.at[:, :, n], load_sem.at[1, b, p]))
     loads = [(b, pltpu.make_async_copy(x, y, z)) for b, x, y, z in loads]
+    def load(b):
+        for at, copy in loads:
+            if at == b:
+                copy.start()
+
     small[0].start()
-    for _, copy in loads:
-        copy.start()
-    for copy in small[1:5]:
-        copy.start()
+    load(0)
     start_barrier()
+    load(1)
 
     S_rows, R_rows = S.reshape(CHUNKS * 1024, LANES), R.reshape(CHUNKS * 1024, LANES)
     S2_rows, R2_rows = S2.reshape(CHUNKS * 1024, LANES), R2.reshape(CHUNKS * 1024, LANES)
@@ -528,6 +570,10 @@
         for at, copy in loads:
             if at == b:
                 copy.wait()
+        if b == 0:
+            load(2)
+            for copy in small[1:5]:
+                copy.start()
         restrict_chunk(b, r, w, pat, A)
         pack_chunk(b, A, S_rows)
         if b == 0:
@@ -596,11 +642,7 @@
             start_copies(halos[s + 1][2:])
 
     planes_to_cells(x_out, G)
-    for b in range(CHUNKS):
-        collect_chunk(b, inv, G, S2_rows)
-        fold_chunk(b, S2_rows)
-        send_chunk(S2, R2, b, s2, r2)
-        keep_own(S2, R2, b)
+    return_all(inv, G, S2, S2_rows, R2, s2, r2)
     for b in range(CHUNKS):
         wait_chunk(R2, b, r2)
         spread_chunk(b, R2_rows, Y)
@@ -613,36 +655,59 @@
             pl.when(sends)(copy.wait_send)
 
 
-def prolong_kernel(y, x, w, pat, out, planes):
-    step = pl.program_id(0)
-
-    def line(n, c):
-        row = step * 6 + n
+def prolong_kernel(y, x, w, pat, out, planes_out, fine, planes, sem, psem):
+    def line(row, c):
         for v in range(6):
             at = (v % 2 * 24 + v // 2) * NI + row
             planes[pl.ds(at, 8, stride=3 * NI), :] = x[pl.ds(row * W + v * 8, 8), :]
         return c
 
-    lax.fori_loop(0, NI // FPA, line, 0)
-
-    def one(k, c):
-        n = pl.multiple_of(k * LANES, LANES)
-        base = pl.multiple_of(k * W, 8)
-        there = bcast_row(pat, pl.ds(k, 1), slice(None)).astype(F32)
-        src = [
-            [y[pl.ds(base + i * 16 + qg * 8, 8), :] * there for qg in range(2)] for i in range(3)
+    lax.fori_loop(0, NI, line, 0)
+    plane_copy = pltpu.make_async_copy(planes, planes_out, psem)
+    plane_copy.start()
+
+    def copies(p):
+        n = pl.ds(pl.multiple_of(p * AGG, AGG), AGG)
+        return [
+            pltpu.make_async_copy(fine.at[j, :, n], out.at[j, :, n], sem.at[p, j])
+            for j in range(3)
         ]
-        for j in range(3):
-            acc = None
-            for i in range(3):
-                wij = jnp.broadcast_to(w[i, j : j + 1, pl.ds(n, LANES)], (8, LANES))
-                terms = [wij * src[i][qg] for qg in range(2)]
-                acc = terms if acc is None else [x + z for x, z in zip(acc, terms)]
-            for qg in range(2):
-                out[j, qg * 8 : qg * 8 + 8, pl.ds(n, LANES)] = acc[qg]
-        return c
-
-    lax.fori_loop(0, NK, one, 0)
+
+    def block(p, c):
+        def some(blk, c):
+            for u in range(4):
+                k = blk * 4 + u
+                at = pl.ds(pl.multiple_of(p * AGG + k * LANES, LANES), LANES)
+                base = pl.multiple_of(k * W, 8)
+                there = bcast_row(pat, pl.ds(p * NK + k, 1), slice(None)).astype(F32)
+                src = [
+                    [y[pl.ds(base + i * 16 + qg * 8, 8), :] * there for qg in range(2)]
+                    for i in range(3)
+                ]
+                for j in range(3):
+                    acc = None
+                    for i in range(3):
+                        wij = jnp.broadcast_to(w[i, j : j + 1, at], (8, LANES))
+                        terms = [wij * src[i][qg] for qg in range(2)]
+                        acc = terms if acc is None else [a + z for a, z in zip(acc, terms)]
+                    for qg in range(2):
+                        fine[j, qg * 8 : qg * 8 + 8, at] = acc[qg]
+            return c
+
+        lax.fori_loop(0, NK // 4, some, 0)
+        for copy in copies(p):
+            copy.start()
+        return c
+
+    lax.fori_loop(0, FPA, block, 0)
+    plane_copy.wait()
+
+    def finish(p, c):
+        for copy in copies(p):
+            copy.wait()
+        return c
+
+    lax.fori_loop(0, FPA, finish, 0)
 
 
 def body(residual, restriction, pattern, cell_aggregate, block_inverse, off_blocks, op_pattern):
@@ -716,22 +781,19 @@
     )
     fine, planes = pl.pallas_call(
         prolong_kernel,
-        grid=(FPA,),
         out_shape=(
             jax.ShapeDtypeStruct((3, NQ, FPA * AGG), F32),
             jax.ShapeDtypeStruct((NQ * 3 * NI, LANES), F32),
         ),
-        in_specs=[
-            vmem,
-            vmem,
-            pl.BlockSpec((3, 3, AGG), lambda p: (0, 0, p)),
-            pl.BlockSpec((NK, LANES), lambda p: (p, 0)),
+        in_specs=[vmem] * 4,
+        out_specs=(hbm, hbm),
+        scratch_shapes=[
+            pltpu.VMEM((3, NQ, FPA * AGG), F32),
+            pltpu.VMEM((NQ * 3 * NI, LANES), F32),
+            pltpu.SemaphoreType.DMA((FPA, 3)),
+            pltpu.SemaphoreType.DMA,
         ],
-        out_specs=(
-            pl.BlockSpec((3, NQ, AGG), lambda p: (0, 0, p)),
-            pl.BlockSpec((NQ * 3 * NI, LANES), lambda p: (0, 0)),
-        ),
-        compiler_params=pltpu.CompilerParams(vmem_limit_bytes=16 * 1024 * 1024),
+        compiler_params=pltpu.CompilerParams(vmem_limit_bytes=24 * 1024 * 1024),
     )(y, x, restriction, pat)
     return planes.reshape(NQ, 3, NI, LANES), fine.transpose(1, 0, 2)
 

time: 77.8 us -> 71.6 us (0.920)
  Pallas kernels: 77 us -> 70.8 us
    pallas_call x1, Pallas kernels: 8.11 us -> 4.76 us  [body(): pl.pallas_call(prolong_kernel, out_shape=(jax.ShapeDtypeStruct((3, NQ, FP...]
    pallas_call x1, Pallas kernels: 68.9 us -> 66 us  [body(): pl.pallas_call(coarse_kernel, out_shape=(jax.ShapeDtypeStruct((NI * W, LA...]
where the time goes in v2:
time: 71.6 us; the launch traced here: 71.5 us
  Pallas kernels  70.8 us (99%)
    pallas_call x1, Pallas kernels, body(): pl.pallas_call(coarse_kernel, out_shape=(jax.ShapeDtypeStruct((NI * W, LA...  66 us
    pallas_call x1, Pallas kernels, body(): pl.pallas_call(prolong_kernel, out_shape=(jax.ShapeDtypeStruct((3, NQ, FP...  4.76 us

profile of v2, /device:TPU:1, one launch (start us, length us, event | category | flops | bytes accessed | tf_op | source)
XLA Modules:
  0.0 71.5 jit_solution(1950802369651509956)
XLA Ops:
  0.6 0.0 copy-start
  0.6 0.0 copy-start.1
  0.7 66.0 %shard_map.86 = (f32[2304,128]{1,0:T(8,128)S(1)}, f32[2304,128]{1,0:T(8,128)S(1)}) custom-call(f32[3,16,49152]{2,1,0:T(8,128)} %bitcast.8, f32[3,3,49152]{2,1,0:T(4,128)} %w.1, s32[384,128]{1,0:T(8,128)} %bitcast.6, s32[48,128]{1,0:T(8,128)} %ca_hbm.1, f32[9,48,128]{2,1,0:T(8,128)} %bitcast.10, f32[36,48,128]{2,1,0:T(8,128)} %bitcast.9, s32[4,48,128]{2,1,0:T(8,128)} %opat_hbm.1), custom_call_target="tpu_custom_call" | custom-call | tf_op jit(solution)/shard_map/pallas_call | solution.py:721
  66.7 0.0 copy-done
  66.7 0.0 copy-done.1
  66.7 4.8 %shard_map.87 = (f32[3,16,49152]{2,1,0:T(8,128)}, f32[2304,128]{1,0:T(8,128)}) custom-call(f32[2304,128]{1,0:T(8,128)S(1)} %get-tuple-element.6.y, f32[2304,128]{1,0:T(8,128)S(1)} %get-tuple-element.7.x, f32[3,3,49152]{2,1,0:T(4,128)S(1)} %copy-done, s32[384,128]{1,0:T(8,128)S(1)} %bitcast.7), custom_call_target="tpu_custom_call" | custom-call | tf_op jit(solution)/shard_map/pallas_call | solution.py:782
Async XLA Ops:
  0.6 66.1 %copy-start = (f32[3,3,49152]{2,1,0:T(4,128)S(1)}, f32[3,3,49152]{2,1,0:T(4,128)}, u32[]{:S(2)}) copy-start(f32[3,3,49152]{2,1,0:T(4,128)} %w.1) | copy-start | bytes 5308420
  0.6 66.1 %copy-start.1 = (s32[49152]{0:T(1024)S(1)}, s32[49152]{0:T(1024)}, u32[]{:S(2)}) copy-start(s32[49152]{0:T(1024)} %param.9) | copy-start | bytes 589828

commit v3 on v2

--- a/solution.py
+++ b/solution.py
@@ -32,19 +32,25 @@
     return jnp.broadcast_to(ref[idx], (8, LANES))
 
 
+def peer_row(row, far, near):
+    z = lax.rem(row // 4 + far, 4)
+    return z * 4 + lax.rem(lax.rem(row, 4) + near, 4)
+
+
 def each_peer(visit):
     row, col = lax.axis_index("row"), lax.axis_index("col")
-    cols = [lax.rem(col + d, 8) for d in range(8)]
-    for other in cols[1:]:
+    cols = [lax.rem(col + d, 8) for d in (2, 6, 1, 3, 5, 7, 4, 0)]
+    for far in (2, 1, 3, 0):
+
+        def one(n, c, far=far):
+            there = peer_row(row, far, 3 - n)
+            for other in cols:
+                visit(there, other)
+            return c
+
+        lax.fori_loop(0, 4 if far else 3, one, 0)
+    for other in cols[:-1]:
         visit(row, other)
-
-    def one(d, c):
-        there = lax.rem(row + d, 16)
-        for other in cols:
-            visit(there, other)
-        return c
-
-    lax.fori_loop(1, 16, one, 0)
 
 
 def start_barrier():
@@ -135,7 +141,7 @@
     lane = lane_ids()
 
     def one(fb, c):
-        for base, h in [(b * 1024 + (fb * 4 + u) * 64, h) for u in range(4) for h in range(2)]:
+        for base, h in [(b * 1024 + (fb * 8 + u) * 64, h) for u in range(8) for h in range(2)]:
             x0 = R2d[pl.ds(base + h, 8, stride=8), :]
             x1 = R2d[pl.ds(base + 2 + h, 8, stride=8), :]
             x2 = R2d[pl.ds(base + 4 + h, 8, stride=8), :]
@@ -144,7 +150,7 @@
             R2d[pl.ds(base + 6 + h, 8, stride=8), :] = jnp.where(lane < 48, six, seven)
         return c
 
-    lax.fori_loop(0, 4, one, 0)
+    lax.fori_loop(0, 2, one, 0)
 
 
 def index_tables(ca, slot_v, odd, inv_v):
@@ -181,16 +187,6 @@
     inv_v[:, 0:NK] = jnp.clip(cell, 0, AGG - 1)
 
 
-def gather_rows(slot, R2d, G):
-    def some(row, c):
-        base = pl.multiple_of(row * LANES, LANES)
-        for u in range(LANES):
-            G[pl.ds(base + u, 1), :] = R2d[pl.ds(slot[row, u], 1), :]
-        return c
-
-    lax.fori_loop(0, NI, some, 0)
-
-
 def solve_block(binv, row, total):
     out = []
     for i in range(3):
@@ -203,26 +199,41 @@
     return out
 
 
-def cells_to_planes(G, odd, rhs, binv, X):
-    def one(blk, c):
-        for u in range(8):
-            row = blk * 8 + u
-            base = pl.multiple_of(row * W, 8)
-            turned = G[pl.ds(pl.multiple_of(row * LANES, LANES), LANES), :].T
-            is_odd = bcast_row(odd, pl.ds(row, 1), slice(None)) == 1
-            total = [[None] * 2 for _ in range(3)]
-            for v in range(6):
-                here = jnp.where(
-                    is_odd, turned[W + v * 8 : W + v * 8 + 8, :], turned[v * 8 : v * 8 + 8, :]
-                )
-                rhs[pl.ds(base + v * 8, 8), :] = here
-                total[v // 2][v % 2] = here
-            new = solve_block(binv, row, total)
-            for v in range(6):
-                X[0, pl.ds(base + W + v * 8, 8), :] = new[v // 2][v % 2]
-        return c
-
-    lax.fori_loop(0, NI // 8, one, 0)
+def slot_copy(blk, n, slot_v, slot, sem):
+    rows = pl.ds(pl.multiple_of(blk * 8, 8), 8)
+    return pltpu.make_async_copy(slot_v.at[rows], slot.at[n], sem.at[n])
+
+
+def gather_cells(slot_v, slot, sem, R2d, G, odd, rhs, binv, X):
+    def finish(row):
+        base = pl.multiple_of(row * W, 8)
+        turned = G[pl.ds(pl.multiple_of(row * LANES, LANES), LANES), :].T
+        is_odd = bcast_row(odd, pl.ds(row, 1), slice(None)) == 1
+        total = [[None] * 2 for _ in range(3)]
+        for v in range(6):
+            here = jnp.where(
+                is_odd, turned[W + v * 8 : W + v * 8 + 8, :], turned[v * 8 : v * 8 + 8, :]
+            )
+            rhs[pl.ds(base + v * 8, 8), :] = here
+            total[v // 2][v % 2] = here
+        new = solve_block(binv, row, total)
+        for v in range(6):
+            X[0, pl.ds(base + W + v * 8, 8), :] = new[v // 2][v % 2]
+
+    def some(two, c):
+        for n in range(2):
+            blk = two * 2 + n
+            slot_copy(blk, n, slot_v, slot, sem).wait()
+            for u in range(8):
+                row = blk * 8 + u
+                base = pl.multiple_of(row * LANES, LANES)
+                for k in range(LANES):
+                    G[pl.ds(base + k, 1), :] = R2d[pl.ds(slot[n, u, k], 1), :]
+                finish(row)
+            pl.when(two < 2)(slot_copy(blk + 2, n, slot_v, slot, sem).start)
+        return c
+
+    lax.fori_loop(0, 3, some, 0)
 
 
 def couplings(off, opat, binv, coup, pc, pb):
@@ -381,14 +392,14 @@
 
 def planes_to_cells(last, G):
     def one(blk, c):
-        for u in range(8):
-            row = blk * 8 + u
+        for u in range(16):
+            row = blk * 16 + u
             x = last[pl.ds(pl.multiple_of(row * W, 8), W), :]
             turned = jnp.concatenate([x, x], axis=0).T
             G[pl.ds(pl.multiple_of(row * LANES, LANES), LANES), 0 : 2 * W] = turned
         return c
 
-    lax.fori_loop(0, NI // 8, one, 0)
+    lax.fori_loop(0, NI // 16, one, 0)
 
 
 def return_all(inv, G, S2, S2_rows, R2, ssem, rsem):
@@ -443,7 +454,9 @@
         pl.when(there != row)(lambda: one(cols[0]))
 
     def peer(d):
-        return lax.rem(row + d, 16)
+        group = d // 4
+        far = jnp.where(group == 0, 2, jnp.where(group == 1, 1, jnp.where(group == 2, 3, 0)))
+        return peer_row(row, far, 3 - lax.rem(d, 4))
 
     for b in range(CHUNKS):
         collect(b, peer(0))
@@ -525,6 +538,7 @@
     inv,
     load_sem,
     small_sem,
+    slot_sem,
     s1,
     r1,
     s2,
@@ -541,7 +555,6 @@
                 (binv_hbm, binv),
                 (off_hbm, off),
                 (opat_hbm, opat),
-                (slot_v, slot),
                 (inv_v, inv),
             ]
         )
@@ -589,16 +602,15 @@
     inv_v[...] = jnp.zeros(inv_v.shape, jnp.int32)
     index_tables(ca, slot_v, odd, inv_v)
     small[5].start()
-    small[6].start()
+    for n in range(2):
+        slot_copy(n, n, slot_v, slot, slot_sem).start()
     couplings(off, opat, binv, coup, pc, pb)
     small[5].wait()
-    small[6].wait()
 
     for b in range(CHUNKS):
         wait_chunk(R, b, r1)
         unfold_chunk(b, R_rows)
-    gather_rows(slot, R_rows, G)
-    cells_to_planes(G, odd, rhs, binv, X)
+    gather_cells(slot_v, slot, slot_sem, R_rows, G, odd, rhs, binv, X)
 
     halos = [halo_copies(s, X, E, H, hs, hr) for s in range(3)]
     start_copies(halos[0][:2])
@@ -630,16 +642,19 @@
             )[1],
             0,
         )
+        if s < 2:
+            pack_edges(s + 1, X, E)
         finish_copies(halos[s][2:])
         correct_edges(s, H, pc, pb, D)
+        if s < 2:
+            for side in range(2):
+                E[side, s + 1] = E[side, s + 1] + D[side]
+            start_copies(halos[s + 1][2:])
         add_edges(0, D, new_at)
         add_edges(2, D, new_at)
         if s < 2:
             start_copies(halos[s + 1][:2])
         add_edges(1, D, new_at)
-        if s < 2:
-            pack_edges(s + 1, X, E)
-            start_copies(halos[s + 1][2:])
 
     planes_to_cells(x_out, G)
     return_all(inv, G, S2, S2_rows, R2, s2, r2)
@@ -751,10 +766,11 @@
             pltpu.VMEM((NI, LANES), jnp.int32),
             pltpu.VMEM((NI, LANES), jnp.int32),
             pltpu.VMEM((ND, LANES), jnp.int32),
-            pltpu.SMEM((NI, LANES), jnp.int32),
+            pltpu.SMEM((2, 8, LANES), jnp.int32),
             pltpu.SMEM((ND, LANES), jnp.int32),
             pltpu.SemaphoreType.DMA((2, CHUNKS, FPA)),
-            pltpu.SemaphoreType.DMA((7,)),
+            pltpu.SemaphoreType.DMA((6,)),
+            pltpu.SemaphoreType.DMA((2,)),
             pltpu.SemaphoreType.DMA((CHUNKS,)),
             pltpu.SemaphoreType.DMA((CHUNKS,)),
             pltpu.SemaphoreType.DMA((CHUNKS,)),

time: 71.6 us -> 68.7 us (0.959)
  Pallas kernels: 70.8 us -> 67.9 us
    pallas_call x1, Pallas kernels: 66 us -> 63.2 us  [body(): pl.pallas_call(coarse_kernel, out_shape=(jax.ShapeDtypeStruct((NI * W, LA...]
where the time goes in v3:
time: 68.7 us; the launch traced here: 68.6 us
  Pallas kernels  67.9 us (99%)
    pallas_call x1, Pallas kernels, body(): pl.pallas_call(coarse_kernel, out_shape=(jax.ShapeDtypeStruct((NI * W, LA...  63.2 us
    pallas_call x1, Pallas kernels, body(): pl.pallas_call(prolong_kernel, out_shape=(jax.ShapeDtypeStruct((3, NQ, FP...  4.76 us

profile of v3, /device:TPU:1, one launch (start us, length us, event | category | flops | bytes accessed | tf_op | source)
XLA Modules:
  0.0 68.6 jit_solution(2074557278254452161)
XLA Ops:
  0.6 0.0 copy-start
  0.6 0.0 copy-start.1
  0.7 63.2 %shard_map.86 = (f32[2304,128]{1,0:T(8,128)S(1)}, f32[2304,128]{1,0:T(8,128)S(1)}) custom-call(f32[3,16,49152]{2,1,0:T(8,128)} %bitcast.8, f32[3,3,49152]{2,1,0:T(4,128)} %w.1, s32[384,128]{1,0:T(8,128)} %bitcast.6, s32[48,128]{1,0:T(8,128)} %ca_hbm.1, f32[9,48,128]{2,1,0:T(8,128)} %bitcast.10, f32[36,48,128]{2,1,0:T(8,128)} %bitcast.9, s32[4,48,128]{2,1,0:T(8,128)} %opat_hbm.1), custom_call_target="tpu_custom_call" | custom-call | tf_op jit(solution)/shard_map/pallas_call | solution.py:736
  63.8 0.0 copy-done
  63.8 0.0 copy-done.1
  63.9 4.8 %shard_map.87 = (f32[3,16,49152]{2,1,0:T(8,128)}, f32[2304,128]{1,0:T(8,128)}) custom-call(f32[2304,128]{1,0:T(8,128)S(1)} %get-tuple-element.6.y, f32[2304,128]{1,0:T(8,128)S(1)} %get-tuple-element.7.x, f32[3,3,49152]{2,1,0:T(4,128)S(1)} %copy-done, s32[384,128]{1,0:T(8,128)S(1)} %bitcast.7), custom_call_target="tpu_custom_call" | custom-call | tf_op jit(solution)/shard_map/pallas_call | solution.py:798
Async XLA Ops:
  0.6 63.2 %copy-start = (f32[3,3,49152]{2,1,0:T(4,128)S(1)}, f32[3,3,49152]{2,1,0:T(4,128)}, u32[]{:S(2)}) copy-start(f32[3,3,49152]{2,1,0:T(4,128)} %w.1) | copy-start | bytes 5308420
  0.6 63.2 %copy-start.1 = (s32[49152]{0:T(1024)S(1)}, s32[49152]{0:T(1024)}, u32[]{:S(2)}) copy-start(s32[49152]{0:T(1024)} %param.9) | copy-start | bytes 589828

commit v4 on v3

--- a/solution.py
+++ b/solution.py
@@ -204,36 +204,41 @@
     return pltpu.make_async_copy(slot_v.at[rows], slot.at[n], sem.at[n])
 
 
-def gather_cells(slot_v, slot, sem, R2d, G, odd, rhs, binv, X):
-    def finish(row):
-        base = pl.multiple_of(row * W, 8)
-        turned = G[pl.ds(pl.multiple_of(row * LANES, LANES), LANES), :].T
-        is_odd = bcast_row(odd, pl.ds(row, 1), slice(None)) == 1
-        total = [[None] * 2 for _ in range(3)]
-        for v in range(6):
-            here = jnp.where(
-                is_odd, turned[W + v * 8 : W + v * 8 + 8, :], turned[v * 8 : v * 8 + 8, :]
-            )
-            rhs[pl.ds(base + v * 8, 8), :] = here
-            total[v // 2][v % 2] = here
-        new = solve_block(binv, row, total)
-        for v in range(6):
-            X[0, pl.ds(base + W + v * 8, 8), :] = new[v // 2][v % 2]
-
+def gather_rows(slot_v, slot, sem, R2d, G):
     def some(two, c):
         for n in range(2):
             blk = two * 2 + n
             slot_copy(blk, n, slot_v, slot, sem).wait()
+            base = pl.multiple_of(blk * 8 * LANES, LANES)
             for u in range(8):
-                row = blk * 8 + u
-                base = pl.multiple_of(row * LANES, LANES)
                 for k in range(LANES):
-                    G[pl.ds(base + k, 1), :] = R2d[pl.ds(slot[n, u, k], 1), :]
-                finish(row)
+                    G[pl.ds(base + u * LANES + k, 1), :] = R2d[pl.ds(slot[n, u, k], 1), :]
             pl.when(two < 2)(slot_copy(blk + 2, n, slot_v, slot, sem).start)
         return c
 
     lax.fori_loop(0, 3, some, 0)
+
+
+def cells_to_planes(G, odd, rhs, binv, X):
+    def one(blk, c):
+        for u in range(8):
+            row = blk * 8 + u
+            base = pl.multiple_of(row * W, 8)
+            turned = G[pl.ds(pl.multiple_of(row * LANES, LANES), LANES), :].T
+            is_odd = bcast_row(odd, pl.ds(row, 1), slice(None)) == 1
+            total = [[None] * 2 for _ in range(3)]
+            for v in range(6):
+                here = jnp.where(
+                    is_odd, turned[W + v * 8 : W + v * 8 + 8, :], turned[v * 8 : v * 8 + 8, :]
+                )
+                rhs[pl.ds(base + v * 8, 8), :] = here
+                total[v // 2][v % 2] = here
+            new = solve_block(binv, row, total)
+            for v in range(6):
+                X[0, pl.ds(base + W + v * 8, 8), :] = new[v // 2][v % 2]
+        return c
+
+    lax.fori_loop(0, NI // 8, one, 0)
 
 
 def couplings(off, opat, binv, coup, pc, pb):
@@ -290,10 +295,10 @@
             E[1, s, v // 2, at : at + 1, :] = turned[LANES - 1 : LANES]
 
 
-def halo_copies(s, X, E, H, hs, hr):
+def halo_copies(s, X, U, E, H, hs, hr):
     row, col = lax.axis_index("row"), lax.axis_index("col")
-    own_first = X.at[s, pl.ds(W, W)]
-    own_last = X.at[s, pl.ds(NI * W, W)]
+    own_first = X.at[s, pl.ds(W, W)] if s == 0 else U.at[s - 1, 0]
+    own_last = X.at[s, pl.ds(NI * W, W)] if s == 0 else U.at[s - 1, 1]
     above = X.at[s, pl.ds(0, W)]
     below = X.at[s, pl.ds((NI + 1) * W, W)]
     table = [
@@ -330,7 +335,7 @@
         pl.when(jnp.logical_not(receives))(clear)
 
 
-def sweep_row(s, row, rhs, binv, coup, X, new_at):
+def row_total(s, row, rhs, coup, X, skip=None):
     base = pl.multiple_of(row * W, 8)
 
     def at(v):
@@ -341,23 +346,38 @@
     right = [pltpu.roll(x, LANES - 1, 1) for x in own]
     total = [[rhs[at(j * 2 + qg), :] for qg in range(2)] for j in range(3)]
     for d in range(4):
-        for k in range(3):
-            near = []
+        if d == skip:
+            continue
+        if d < 2:
+            near = [X[s, at(v + 12 * d), :] for v in range(6)]
+        else:
+            near = left if d == 2 else right
+        total = less_direction(d, row, coup, near, total)
+    return total
+
+
+def less_direction(d, row, coup, near, total):
+    total = [list(t) for t in total]
+    for k in range(3):
+        for j in range(3):
+            coef = bcast_row(coup, d * 9 + j * 3 + k, pl.ds(row, 1), slice(None))
             for qg in range(2):
-                v = k * 2 + qg
-                if d == 0:
-                    near.append(X[s, at(v), :])
-                elif d == 1:
-                    near.append(X[s, at(v + 12), :])
-                else:
-                    near.append((left if d == 2 else right)[v])
-            for j in range(3):
-                coef = bcast_row(coup, d * 9 + j * 3 + k, pl.ds(row, 1), slice(None))
-                for qg in range(2):
-                    total[j][qg] = total[j][qg] - coef * near[qg]
-    new = solve_block(binv, row, total)
+                total[j][qg] = total[j][qg] - coef * near[k * 2 + qg]
+    return total
+
+
+def edge_lanes(blk, n, D):
+    lane = lane_ids()
+    here = lane == lax.broadcasted_iota(jnp.int32, (8, LANES), 0) + 8 * n
+    out = []
     for v in range(6):
-        new_at(row, v)[...] = new[v // 2][v % 2]
+        at = v % 2 * 3 + blk
+        ends = []
+        for side in range(2):
+            line = bcast_row(D, side, v // 2, slice(at, at + 1), slice(None))
+            ends.append(jnp.sum(jnp.where(here, line, 0.0), axis=1, keepdims=True))
+        out.append(jnp.where(lane == 0, ends[0], jnp.where(lane == LANES - 1, ends[1], 0.0)))
+    return out
 
 
 def correct_edges(s, H, pc, pb, D):
@@ -510,9 +530,9 @@
     opat_hbm,
     x_out,
     Y,
-    r,
     w,
     pat,
+    r,
     ca,
     binv,
     off,
@@ -525,6 +545,7 @@
     G,
     rhs,
     X,
+    U,
     E,
     H,
     D,
@@ -539,6 +560,7 @@
     load_sem,
     small_sem,
     slot_sem,
+    inv_sem,
     s1,
     r1,
     s2,
@@ -555,7 +577,6 @@
                 (binv_hbm, binv),
                 (off_hbm, off),
                 (opat_hbm, opat),
-                (inv_v, inv),
             ]
         )
     ]
@@ -601,21 +622,24 @@
     pb[...] = jnp.zeros(pb.shape, F32)
     inv_v[...] = jnp.zeros(inv_v.shape, jnp.int32)
     index_tables(ca, slot_v, odd, inv_v)
-    small[5].start()
+    inv_copy = pltpu.make_async_copy(inv_v, inv, inv_sem)
+    inv_copy.start()
     for n in range(2):
         slot_copy(n, n, slot_v, slot, slot_sem).start()
     couplings(off, opat, binv, coup, pc, pb)
-    small[5].wait()
+    inv_copy.wait()
 
     for b in range(CHUNKS):
         wait_chunk(R, b, r1)
         unfold_chunk(b, R_rows)
-    gather_cells(slot_v, slot, slot_sem, R_rows, G, odd, rhs, binv, X)
-
-    halos = [halo_copies(s, X, E, H, hs, hr) for s in range(3)]
+    gather_rows(slot_v, slot, slot_sem, R_rows, G)
+    cells_to_planes(G, odd, rhs, binv, X)
+
+    halos = [halo_copies(s, X, U, E, H, hs, hr) for s in range(3)]
     start_copies(halos[0][:2])
     pack_edges(0, X, E)
     start_copies(halos[0][2:])
+    ends = ((0, 0, 0), (NI - 1, 2, 15))
     for s in range(3):
         if s < 2:
 
@@ -628,33 +652,35 @@
 
         def inner(two, c, s=s, new_at=new_at):
             for u in range(2):
-                sweep_row(s, 1 + two * 2 + u, rhs, binv, coup, X, new_at)
+                row = 1 + two * 2 + u
+                new = solve_block(binv, row, row_total(s, row, rhs, coup, X))
+                for v in range(6):
+                    new_at(row, v)[...] = new[v // 2][v % 2]
             return c
 
         lax.fori_loop(0, (NI - 2) // 2, inner, 0)
+        totals = [row_total(s, row, rhs, coup, X, skip=d) for d, (row, _, _) in enumerate(ends)]
         finish_copies(halos[s][:2])
-        lax.fori_loop(
-            0,
-            2,
-            lambda n, c, s=s, new_at=new_at: (
-                sweep_row(s, n * (NI - 1), rhs, binv, coup, X, new_at),
-                c,
-            )[1],
-            0,
-        )
-        if s < 2:
-            pack_edges(s + 1, X, E)
+        new = []
+        for d, (row, _, _) in enumerate(ends):
+            near = [X[s, pl.ds((row + 2 * d) * W + v * 8, 8), :] for v in range(6)]
+            new.append(solve_block(binv, row, less_direction(d, row, coup, near, totals[d])))
+            for v in range(6):
+                new_at(row, v)[...] = new[d][v // 2][v % 2]
         finish_copies(halos[s][2:])
         correct_edges(s, H, pc, pb, D)
         if s < 2:
+            for d, (_, blk, n) in enumerate(ends):
+                more = edge_lanes(blk, n, D)
+                for v in range(6):
+                    U[s, d, v * 8 : v * 8 + 8, :] = new[d][v // 2][v % 2] + more[v]
+            start_copies(halos[s + 1][:2])
+            pack_edges(s + 1, X, E)
             for side in range(2):
                 E[side, s + 1] = E[side, s + 1] + D[side]
             start_copies(halos[s + 1][2:])
-        add_edges(0, D, new_at)
-        add_edges(2, D, new_at)
-        if s < 2:
-            start_copies(halos[s + 1][:2])
-        add_edges(1, D, new_at)
+        for blk in range(3):
+            add_edges(blk, D, new_at)
 
     planes_to_cells(x_out, G)
     return_all(inv, G, S2, S2_rows, R2, s2, r2)
@@ -733,18 +759,18 @@
     msg = pltpu.VMEM((CHUNKS, ND, 8, LANES), F32)
     plane = pltpu.VMEM((NI * W, LANES), F32)
     edge = pltpu.VMEM((2, 3, 3, 8, LANES), F32)
-    x, y = pl.pallas_call(
+    x, y, held, held_pat = pl.pallas_call(
         coarse_kernel,
         out_shape=(
             jax.ShapeDtypeStruct((NI * W, LANES), F32),
             jax.ShapeDtypeStruct((NK * W, LANES), F32),
+            jax.ShapeDtypeStruct((3, 3, FPA * AGG), F32),
+            jax.ShapeDtypeStruct((384, LANES), jnp.int32),
         ),
         in_specs=[hbm] * 7,
-        out_specs=(vmem, vmem),
+        out_specs=(vmem,) * 4,
         scratch_shapes=[
             pltpu.VMEM((3, NQ, FPA * AGG), F32),
-            pltpu.VMEM((3, 3, FPA * AGG), F32),
-            pltpu.VMEM((384, LANES), jnp.int32),
             pltpu.VMEM((NI, LANES), jnp.int32),
             pltpu.VMEM((9, NI, LANES), F32),
             pltpu.VMEM((36, NI, LANES), F32),
@@ -757,6 +783,7 @@
             pltpu.VMEM((AGG, LANES), F32),
             plane,
             pltpu.VMEM((3, (NI + 2) * W, LANES), F32),
+            pltpu.VMEM((2, 2, W, LANES), F32),
             edge,
             edge,
             pltpu.VMEM((2, 3, 8, LANES), F32),
@@ -769,8 +796,9 @@
             pltpu.SMEM((2, 8, LANES), jnp.int32),
             pltpu.SMEM((ND, LANES), jnp.int32),
             pltpu.SemaphoreType.DMA((2, CHUNKS, FPA)),
-            pltpu.SemaphoreType.DMA((6,)),
+            pltpu.SemaphoreType.DMA((5,)),
             pltpu.SemaphoreType.DMA((2,)),
+            pltpu.SemaphoreType.DMA,
             pltpu.SemaphoreType.DMA((CHUNKS,)),
             pltpu.SemaphoreType.DMA((CHUNKS,)),
             pltpu.SemaphoreType.DMA((CHUNKS,)),
@@ -810,7 +838,7 @@
             pltpu.SemaphoreType.DMA,
         ],
         compiler_params=pltpu.CompilerParams(vmem_limit_bytes=24 * 1024 * 1024),
-    )(y, x, restriction, pat)
+    )(y, x, held, held_pat)
     return planes.reshape(NQ, 3, NI, LANES), fine.transpose(1, 0, 2)
 
 

time: 68.7 us -> 67.8 us (0.987)
  Pallas kernels: 67.9 us -> 67 us
    pallas_call x1, Pallas kernels: 63.2 us -> 62.3 us  [body(): pl.pallas_call(coarse_kernel, out_shape=(jax.ShapeDtypeStruct((NI * W, LA...]
where the time goes in v4:
time: 67.8 us; the launch traced here: 67.7 us
  Pallas kernels  67 us (99%)
    pallas_call x1, Pallas kernels, body(): pl.pallas_call(coarse_kernel, out_shape=(jax.ShapeDtypeStruct((NI * W, LA...  62.3 us
    pallas_call x1, Pallas kernels, body(): pl.pallas_call(prolong_kernel, out_shape=(jax.ShapeDtypeStruct((3, NQ, FP...  4.76 us

profile of v4, /device:TPU:1, one launch (start us, length us, event | category | flops | bytes accessed | tf_op | source)
XLA Modules:
  0.0 67.7 jit_solution(8167485325400190701)
XLA Ops:
  0.6 62.3 %shard_map.86 = (f32[2304,128]{1,0:T(8,128)S(1)}, f32[2304,128]{1,0:T(8,128)S(1)}, f32[3,3,49152]{2,1,0:T(4,128)S(1)}, s32[384,128]{1,0:T(8,128)S(1)}) custom-call(f32[3,16,49152]{2,1,0:T(8,128)} %bitcast.6, f32[3,3,49152]{2,1,0:T(4,128)} %w_hbm.1, s32[384,128]{1,0:T(8,128)} %bitcast.9, s32[48,128]{1,0:T(8,128)} %ca_hbm.1, f32[9,48,128]{2,1,0:T(8,128)} %bitcast.8, ...), custom_call_target="tpu_custom_call" | custom-call | tf_op jit(solution)/shard_map/pallas_call | solution.py:762
  62.9 4.8 %shard_map.87 = (f32[3,16,49152]{2,1,0:T(8,128)}, f32[2304,128]{1,0:T(8,128)}) custom-call(f32[2304,128]{1,0:T(8,128)S(1)} %get-tuple-element.8.y, f32[2304,128]{1,0:T(8,128)S(1)} %get-tuple-element.9.x, f32[3,3,49152]{2,1,0:T(4,128)S(1)} %get-tuple-element.10.w, s32[384,128]{1,0:T(8,128)S(1)} %get-tuple-element.11.pat), custom_call_target="tpu_custom_call" | custom-call | tf_op jit(solution)/shard_map/pallas_call | solution.py:826

commit v5 on v4

--- a/solution.py
+++ b/solution.py
@@ -204,27 +204,18 @@
     return pltpu.make_async_copy(slot_v.at[rows], slot.at[n], sem.at[n])
 
 
-def gather_rows(slot_v, slot, sem, R2d, G):
-    def some(two, c):
-        for n in range(2):
-            blk = two * 2 + n
-            slot_copy(blk, n, slot_v, slot, sem).wait()
-            base = pl.multiple_of(blk * 8 * LANES, LANES)
-            for u in range(8):
-                for k in range(LANES):
-                    G[pl.ds(base + u * LANES + k, 1), :] = R2d[pl.ds(slot[n, u, k], 1), :]
-            pl.when(two < 2)(slot_copy(blk + 2, n, slot_v, slot, sem).start)
-        return c
-
-    lax.fori_loop(0, 3, some, 0)
-
-
-def cells_to_planes(G, odd, rhs, binv, X):
-    def one(blk, c):
+def gather_cells(slot_v, slot, sem, R2d, near, odd, rhs, binv, X):
+    def fetch(blk, n):
+        slot_copy(blk, n, slot_v, slot, sem).wait()
+        for u in range(8):
+            for k in range(LANES):
+                near[n][pl.ds(u * LANES + k, 1), :] = R2d[pl.ds(slot[n, u, k], 1), :]
+
+    def planes(blk, n):
         for u in range(8):
             row = blk * 8 + u
             base = pl.multiple_of(row * W, 8)
-            turned = G[pl.ds(pl.multiple_of(row * LANES, LANES), LANES), :].T
+            turned = near[n][pl.ds(u * LANES, LANES), :].T
             is_odd = bcast_row(odd, pl.ds(row, 1), slice(None)) == 1
             total = [[None] * 2 for _ in range(3)]
             for v in range(6):
@@ -236,9 +227,25 @@
             new = solve_block(binv, row, total)
             for v in range(6):
                 X[0, pl.ds(base + W + v * 8, 8), :] = new[v // 2][v % 2]
+
+    fetch(0, 0)
+    slot_copy(2, 0, slot_v, slot, sem).start()
+
+    def some(two, c):
+        blk = two * 2 + 1
+        fetch(blk, 1)
+        planes(blk - 1, 0)
+        slot_copy(jnp.minimum(blk + 2, 5), 1, slot_v, slot, sem).start()
+        fetch(blk + 1, 0)
+        planes(blk, 1)
+        slot_copy(jnp.minimum(blk + 3, 5), 0, slot_v, slot, sem).start()
         return c
 
-    lax.fori_loop(0, NI // 8, one, 0)
+    lax.fori_loop(0, 2, some, 0)
+    fetch(5, 1)
+    planes(4, 0)
+    slot_copy(5, 0, slot_v, slot, sem).wait()
+    planes(5, 1)
 
 
 def couplings(off, opat, binv, coup, pc, pb):
@@ -282,17 +289,31 @@
     lax.fori_loop(0, 9, mask, 0)
 
 
-def pack_edges(s, X, E):
+def pack_edges(s, X, E, ends=True):
+    zero = jnp.zeros((8, LANES), F32)
     for blk in range(3):
         for v in range(6):
+            rows = [blk * 16 + n for n in range(16)]
             parts = [
-                X[s, (blk * 16 + n + 1) * W + v * 8 : (blk * 16 + n + 1) * W + v * 8 + 8, :]
-                for n in range(16)
+                X[s, (row + 1) * W + v * 8 : (row + 1) * W + v * 8 + 8, :]
+                if ends or 0 < row < NI - 1
+                else zero
+                for row in rows
             ]
             turned = jnp.concatenate(parts, axis=0).T
             at = v % 2 * 3 + blk
             E[0, s, v // 2, at : at + 1, :] = turned[0:1]
             E[1, s, v // 2, at : at + 1, :] = turned[LANES - 1 : LANES]
+
+
+def patch_edges(s, blk, n, new, E):
+    here = lane_ids() == lax.broadcasted_iota(jnp.int32, (8, LANES), 0) + 8 * n
+    for v in range(6):
+        at = v % 2 * 3 + blk
+        x = new[v // 2][v % 2]
+        for side, column in enumerate((x[:, 0:1], x[:, LANES - 1 : LANES])):
+            line = jnp.sum(jnp.where(here, column, 0.0), axis=0, keepdims=True)
+            E[side, s, v // 2, at : at + 1, :] = E[side, s, v // 2, at : at + 1, :] + line
 
 
 def halo_copies(s, X, U, E, H, hs, hr):
@@ -410,16 +431,28 @@
             ref[...] = ref[...] + turned[n * 8 : n * 8 + 8]
 
 
-def planes_to_cells(last, G):
-    def one(blk, c):
-        for u in range(16):
-            row = blk * 16 + u
-            x = last[pl.ds(pl.multiple_of(row * W, 8), W), :]
-            turned = jnp.concatenate([x, x], axis=0).T
-            G[pl.ds(pl.multiple_of(row * LANES, LANES), LANES), 0 : 2 * W] = turned
-        return c
-
-    lax.fori_loop(0, NI // 16, one, 0)
+def planes_to_cells(row, last, G):
+    x = last[pl.ds(pl.multiple_of(row * W, 8), W), :]
+    turned = jnp.concatenate([x, x], axis=0).T
+    G[pl.ds(pl.multiple_of(row * LANES, LANES), LANES), 0 : 2 * W] = turned
+
+
+def correct_cells(D, G):
+    lane = lane_ids()
+    sub = lax.broadcasted_iota(jnp.int32, (8, LANES), 0)
+    group = lax.shift_right_logical(lane, 3)
+    for side, column in ((0, 0), (1, LANES - 1)):
+        for blk in range(3):
+            for half in range(2):
+                source = (lane & 7) + (sub + half * 8) * 8
+                acc = jnp.zeros((8, LANES), F32)
+                for v in range(6):
+                    at = v % 2 * 3 + blk
+                    line = bcast_row(D, side, v // 2, slice(at, at + 1), slice(None))
+                    moved = jnp.take_along_axis(line, source, axis=1)
+                    acc = jnp.where((group == v) | (group == v + 6), moved, acc)
+                rows = pl.ds((blk * 16 + half * 8) * LANES + column, 8, stride=LANES)
+                G[rows, :] = G[rows, :] + acc
 
 
 def return_all(inv, G, S2, S2_rows, R2, ssem, rsem):
@@ -543,6 +576,8 @@
     S2,
     R2,
     G,
+    G0,
+    G1,
     rhs,
     X,
     U,
@@ -632,8 +667,7 @@
     for b in range(CHUNKS):
         wait_chunk(R, b, r1)
         unfold_chunk(b, R_rows)
-    gather_rows(slot_v, slot, slot_sem, R_rows, G)
-    cells_to_planes(G, odd, rhs, binv, X)
+    gather_cells(slot_v, slot, slot_sem, R_rows, (G0, G1), odd, rhs, binv, X)
 
     halos = [halo_copies(s, X, U, E, H, hs, hr) for s in range(3)]
     start_copies(halos[0][:2])
@@ -660,6 +694,16 @@
 
         lax.fori_loop(0, (NI - 2) // 2, inner, 0)
         totals = [row_total(s, row, rhs, coup, X, skip=d) for d, (row, _, _) in enumerate(ends)]
+        if s < 2:
+            pack_edges(s + 1, X, E, ends=False)
+        else:
+
+            def turn(part, c):
+                for u in range(23):
+                    planes_to_cells(1 + part * 23 + u, x_out, G)
+                return c
+
+            lax.fori_loop(0, 2, turn, 0)
         finish_copies(halos[s][:2])
         new = []
         for d, (row, _, _) in enumerate(ends):
@@ -667,23 +711,31 @@
             new.append(solve_block(binv, row, less_direction(d, row, coup, near, totals[d])))
             for v in range(6):
                 new_at(row, v)[...] = new[d][v // 2][v % 2]
+        if s < 2:
+            for d, (_, blk, n) in enumerate(ends):
+                patch_edges(s + 1, blk, n, new[d], E)
+        else:
+            for row in (0, NI - 1):
+                planes_to_cells(row, x_out, G)
         finish_copies(halos[s][2:])
         correct_edges(s, H, pc, pb, D)
         if s < 2:
+            for side in range(2):
+                E[side, s + 1] = E[side, s + 1] + D[side]
+            start_copies(halos[s + 1][2:])
             for d, (_, blk, n) in enumerate(ends):
                 more = edge_lanes(blk, n, D)
                 for v in range(6):
                     U[s, d, v * 8 : v * 8 + 8, :] = new[d][v // 2][v % 2] + more[v]
             start_copies(halos[s + 1][:2])
-            pack_edges(s + 1, X, E)
-            for side in range(2):
-                E[side, s + 1] = E[side, s + 1] + D[side]
-            start_copies(halos[s + 1][2:])
-        for blk in range(3):
-            add_edges(blk, D, new_at)
-
-    planes_to_cells(x_out, G)
+            for blk in range(3):
+                add_edges(blk, D, new_at)
+        else:
+            correct_cells(D, G)
+
     return_all(inv, G, S2, S2_rows, R2, s2, r2)
+    for blk in range(3):
+        add_edges(blk, D, new_at)
     for b in range(CHUNKS):
         wait_chunk(R2, b, r2)
         spread_chunk(b, R2_rows, Y)
@@ -781,6 +833,8 @@
             msg,
             msg,
             pltpu.VMEM((AGG, LANES), F32),
+            pltpu.VMEM((8 * LANES, LANES), F32),
+            pltpu.VMEM((8 * LANES, LANES), F32),
             plane,
             pltpu.VMEM((3, (NI + 2) * W, LANES), F32),
             pltpu.VMEM((2, 2, W, LANES), F32),

time: 67.8 us -> 66.1 us (0.975)
  Pallas kernels: 67 us -> 65.3 us
    pallas_call x1, Pallas kernels: 62.3 us -> 60.5 us  [body(): pl.pallas_call(coarse_kernel, out_shape=(jax.ShapeDtypeStruct((NI * W, LA...]
where the time goes in v5:
time: 66.1 us; the launch traced here: 65.9 us
  Pallas kernels  65.3 us (99%)
    pallas_call x1, Pallas kernels, body(): pl.pallas_call(coarse_kernel, out_shape=(jax.ShapeDtypeStruct((NI * W, LA...  60.5 us
    pallas_call x1, Pallas kernels, body(): pl.pallas_call(prolong_kernel, out_shape=(jax.ShapeDtypeStruct((3, NQ, FP...  4.76 us

profile of v5, /device:TPU:1, one launch (start us, length us, event | category | flops | bytes accessed | tf_op | source)
XLA Modules:
  0.0 65.9 jit_solution(11489682350024370355)
XLA Ops:
  0.6 60.5 %shard_map.86 = (f32[2304,128]{1,0:T(8,128)S(1)}, f32[2304,128]{1,0:T(8,128)S(1)}, f32[3,3,49152]{2,1,0:T(4,128)S(1)}, s32[384,128]{1,0:T(8,128)S(1)}) custom-call(f32[3,16,49152]{2,1,0:T(8,128)} %bitcast.6, f32[3,3,49152]{2,1,0:T(4,128)} %w_hbm.1, s32[384,128]{1,0:T(8,128)} %bitcast.9, s32[48,128]{1,0:T(8,128)} %ca_hbm.1, f32[9,48,128]{2,1,0:T(8,128)} %bitcast.8, ...), custom_call_target="tpu_custom_call" | custom-call | tf_op jit(solution)/shard_map/pallas_call | solution.py:814
  61.2 4.8 %shard_map.87 = (f32[3,16,49152]{2,1,0:T(8,128)}, f32[2304,128]{1,0:T(8,128)}) custom-call(f32[2304,128]{1,0:T(8,128)S(1)} %get-tuple-element.8.y, f32[2304,128]{1,0:T(8,128)S(1)} %get-tuple-element.9.x, f32[3,3,49152]{2,1,0:T(4,128)S(1)} %get-tuple-element.10.w, s32[384,128]{1,0:T(8,128)S(1)} %get-tuple-element.11.pat), custom_call_target="tpu_custom_call" | custom-call | tf_op jit(solution)/shard_map/pallas_call | solution.py:880

commit v6 on v5

--- a/solution.py
+++ b/solution.py
@@ -199,21 +199,52 @@
     return out
 
 
+def early_edges(slot, R2d, T, edge_odd, pb, D, E):
+    for side, column in ((0, 0), (1, LANES - 1)):
+        for row in range(NI):
+            T[side * 64 + row : side * 64 + row + 1, :] = R2d[pl.ds(slot[row, column], 1), :]
+    turned = T[...].T
+    is_odd = bcast_row(edge_odd, slice(0, 1), slice(None)) > 0.5
+    lane = lane_ids()
+    here = lax.broadcasted_iota(jnp.int32, (8, LANES), 0) == (lane & 7)
+    D[...] = jnp.zeros(D.shape, F32)
+    for v in range(6):
+        at = v * 8
+        cells = jnp.where(is_odd, turned[W + at : W + at + 8, :], turned[at : at + 8, :])
+        for side in range(2):
+            for blk in range(3):
+                source = lax.shift_right_logical(lane, 3) + (side * 64 + blk * 16)
+                moved = jnp.where(here, jnp.take_along_axis(cells, source, axis=1), 0.0)
+                n = v % 2 * 3 + blk
+                D[side, v // 2, n : n + 1, :] = jnp.sum(moved, axis=0, keepdims=True)
+    for side in range(2):
+        for i in range(3):
+            acc = None
+            for j in range(3):
+                term = pb[side, i * 3 + j] * D[side, j]
+                acc = term if acc is None else acc + term
+            E[side, 0, i] = acc
+
+
 def slot_copy(blk, n, slot_v, slot, sem):
     rows = pl.ds(pl.multiple_of(blk * 8, 8), 8)
     return pltpu.make_async_copy(slot_v.at[rows], slot.at[n], sem.at[n])
 
 
-def gather_cells(slot_v, slot, sem, R2d, near, odd, rhs, binv, X):
-    def fetch(blk, n):
-        slot_copy(blk, n, slot_v, slot, sem).wait()
+def nth_block(n):
+    return jnp.where(n == 0, 0, jnp.where(n == 1, 5, n - 1))
+
+
+def gather_cells(slot_v, slot, sem, R2d, near, odd, rhs, binv, X, ends_done):
+    def fetch(step, n):
+        slot_copy(nth_block(step), n, slot_v, slot, sem).wait()
         for u in range(8):
             for k in range(LANES):
                 near[n][pl.ds(u * LANES + k, 1), :] = R2d[pl.ds(slot[n, u, k], 1), :]
 
-    def planes(blk, n):
+    def planes(step, n):
         for u in range(8):
-            row = blk * 8 + u
+            row = nth_block(step) * 8 + u
             base = pl.multiple_of(row * W, 8)
             turned = near[n][pl.ds(u * LANES, LANES), :].T
             is_odd = bcast_row(odd, pl.ds(row, 1), slice(None)) == 1
@@ -229,22 +260,23 @@
                 X[0, pl.ds(base + W + v * 8, 8), :] = new[v // 2][v % 2]
 
     fetch(0, 0)
-    slot_copy(2, 0, slot_v, slot, sem).start()
+    slot_copy(nth_block(2), 0, slot_v, slot, sem).start()
 
     def some(two, c):
         blk = two * 2 + 1
         fetch(blk, 1)
         planes(blk - 1, 0)
-        slot_copy(jnp.minimum(blk + 2, 5), 1, slot_v, slot, sem).start()
+        slot_copy(nth_block(jnp.minimum(blk + 2, 5)), 1, slot_v, slot, sem).start()
         fetch(blk + 1, 0)
         planes(blk, 1)
-        slot_copy(jnp.minimum(blk + 3, 5), 0, slot_v, slot, sem).start()
+        slot_copy(nth_block(jnp.minimum(blk + 3, 5)), 0, slot_v, slot, sem).start()
+        pl.when(two == 0)(ends_done)
         return c
 
     lax.fori_loop(0, 2, some, 0)
     fetch(5, 1)
     planes(4, 0)
-    slot_copy(5, 0, slot_v, slot, sem).wait()
+    slot_copy(nth_block(5), 0, slot_v, slot, sem).wait()
     planes(5, 1)
 
 
@@ -578,6 +610,8 @@
     G,
     G0,
     G1,
+    T,
+    edge_odd,
     rhs,
     X,
     U,
@@ -591,10 +625,12 @@
     odd,
     inv_v,
     slot,
+    ring,
     inv,
     load_sem,
     small_sem,
     slot_sem,
+    ring_sem,
     inv_sem,
     s1,
     r1,
@@ -659,20 +695,37 @@
     index_tables(ca, slot_v, odd, inv_v)
     inv_copy = pltpu.make_async_copy(inv_v, inv, inv_sem)
     inv_copy.start()
+    all_slots = pltpu.make_async_copy(slot_v, slot, slot_sem)
+    all_slots.start()
     for n in range(2):
-        slot_copy(n, n, slot_v, slot, slot_sem).start()
+        slot_copy(nth_block(n), n, slot_v, ring, ring_sem).start()
+    both = jnp.concatenate([odd[...].astype(F32), jnp.zeros((16, LANES), F32)], axis=0)
+    turned = jnp.concatenate([both, both], axis=0).T
+    low = lax.broadcasted_iota(jnp.int32, (1, LANES), 1) < 64
+    edge_odd[0:1, :] = jnp.where(low, turned[0:1], turned[LANES - 1 : LANES])
+    T[...] = jnp.zeros(T.shape, F32)
     couplings(off, opat, binv, coup, pc, pb)
     inv_copy.wait()
+    all_slots.wait()
 
     for b in range(CHUNKS):
         wait_chunk(R, b, r1)
         unfold_chunk(b, R_rows)
-    gather_cells(slot_v, slot, slot_sem, R_rows, (G0, G1), odd, rhs, binv, X)
-
     halos = [halo_copies(s, X, U, E, H, hs, hr) for s in range(3)]
-    start_copies(halos[0][:2])
-    pack_edges(0, X, E)
+    early_edges(slot, R_rows, T, edge_odd, pb, D, E)
     start_copies(halos[0][2:])
+    gather_cells(
+        slot_v,
+        ring,
+        ring_sem,
+        R_rows,
+        (G0, G1),
+        odd,
+        rhs,
+        binv,
+        X,
+        lambda: start_copies(halos[0][:2]),
+    )
     ends = ((0, 0, 0), (NI - 1, 2, 15))
     for s in range(3):
         if s < 2:
@@ -835,6 +888,8 @@
             pltpu.VMEM((AGG, LANES), F32),
             pltpu.VMEM((8 * LANES, LANES), F32),
             pltpu.VMEM((8 * LANES, LANES), F32),
+            pltpu.VMEM((LANES, LANES), F32),
+            pltpu.VMEM((8, LANES), F32),
             plane,
             pltpu.VMEM((3, (NI + 2) * W, LANES), F32),
             pltpu.VMEM((2, 2, W, LANES), F32),
@@ -847,10 +902,12 @@
             pltpu.VMEM((NI, LANES), jnp.int32),
             pltpu.VMEM((NI, LANES), jnp.int32),
             pltpu.VMEM((ND, LANES), jnp.int32),
+            pltpu.SMEM((NI, LANES), jnp.int32),
             pltpu.SMEM((2, 8, LANES), jnp.int32),
             pltpu.SMEM((ND, LANES), jnp.int32),
             pltpu.SemaphoreType.DMA((2, CHUNKS, FPA)),
             pltpu.SemaphoreType.DMA((5,)),
+            pltpu.SemaphoreType.DMA,
             pltpu.SemaphoreType.DMA((2,)),
             pltpu.SemaphoreType.DMA,
             pltpu.SemaphoreType.DMA((CHUNKS,)),

time: 66.1 us -> 65.6 us (level)
  no operation moved by 1% of the time
where the time goes in v6:
time: 65.6 us; the launch traced here: 65.5 us
  Pallas kernels  64.9 us (99%)
    pallas_call x1, Pallas kernels, body(): pl.pallas_call(coarse_kernel, out_shape=(jax.ShapeDtypeStruct((NI * W, LA...  60.1 us
    pallas_call x1, Pallas kernels, body(): pl.pallas_call(prolong_kernel, out_shape=(jax.ShapeDtypeStruct((3, NQ, FP...  4.76 us

profile of v6, /device:TPU:1, one launch (start us, length us, event | category | flops | bytes accessed | tf_op | source)
XLA Modules:
  0.0 65.5 jit_solution(10985553862764193375)
XLA Ops:
  0.6 60.1 %shard_map.86 = (f32[2304,128]{1,0:T(8,128)S(1)}, f32[2304,128]{1,0:T(8,128)S(1)}, f32[3,3,49152]{2,1,0:T(4,128)S(1)}, s32[384,128]{1,0:T(8,128)S(1)}) custom-call(f32[3,16,49152]{2,1,0:T(8,128)} %bitcast.6, f32[3,3,49152]{2,1,0:T(4,128)} %w_hbm.1, s32[384,128]{1,0:T(8,128)} %bitcast.9, s32[48,128]{1,0:T(8,128)} %ca_hbm.1, f32[9,48,128]{2,1,0:T(8,128)} %bitcast.8, ...), custom_call_target="tpu_custom_call" | custom-call | tf_op jit(solution)/shard_map/pallas_call | solution.py:867
  60.7 4.8 %shard_map.87 = (f32[3,16,49152]{2,1,0:T(8,128)}, f32[2304,128]{1,0:T(8,128)}) custom-call(f32[2304,128]{1,0:T(8,128)S(1)} %get-tuple-element.8.y, f32[2304,128]{1,0:T(8,128)S(1)} %get-tuple-element.9.x, f32[3,3,49152]{2,1,0:T(4,128)S(1)} %get-tuple-element.10.w, s32[384,128]{1,0:T(8,128)S(1)} %get-tuple-element.11.pat), custom_call_target="tpu_custom_call" | custom-call | tf_op jit(solution)/shard_map/pallas_call | solution.py:937
